TPU v7x, 32 devices: a whole 2x2x4 slice. The times are simulated.
32 devices in a mesh: task: 16 (over z, x, core), tensor: 2 (over y).
Axes of the slice: x: 2, y: 2, z: 4, core: 2. Of those that a mesh axis runs over, the one named last changes fastest.
Arguments:
- inputs: bfloat16 [2048, 4096], P('task', 'tensor'), may hold values from -6 to 6
- targets: bfloat16 [2048, 4096], P('task', 'tensor'), may hold values from -6 to 6
- queries: bfloat16 [2048, 2048], P('task', 'tensor'), may hold values from -120 to 120
- key_rows: bfloat16 [2048, 2048], P('task', 'tensor'), may hold values from -4 to 4
- value_weight: bfloat16 [4096, 2048], P(None, 'tensor'), may hold values from -0.09375 to 0.09375
- output_weight: bfloat16 [2048, 4096], P('tensor'), may hold values from -0.125 to 0.125
- splits: int32 [16], P('task'), may hold values from 32 to 96
Outputs:
- meta_value: float32 [4096, 2048], P('task', 'tensor')
- meta_output: float32 [2048, 4096], P('tensor', 'task')
Inputs may be any that keep to these rules, and one draw needn't show every extreme that they name: `splits`: support and query parts of every task are both nonempty.
All inputs are finite; a program needn't handle non-finite values.
Results may differ from a plain program's by a relative error of at most 0.025.
Values may be sent and summed in bfloat16 or wider, within the bound.
A program may use at most 128 MiB of HBM per device.

v0:
```python
import functools

import jax
import jax.numpy as jnp
from jax import lax
from jax.experimental import pallas as pl
from jax.experimental.pallas import tpu as pltpu
from jax.sharding import PartitionSpec as P

HD = 128
BF = jnp.bfloat16
F32 = jnp.float32

step_rate = 0.25


def normed_rows(inputs):
    values = inputs.astype(F32)
    scale = lax.rsqrt(jnp.mean(values * values, axis=-1, keepdims=True) + 1e-05)
    return (values * scale).astype(BF)


def attention_probs(queries, key_rows, heads):
    length = queries.shape[0]
    query_h = queries.reshape(length, heads, -1)
    key_h = key_rows.reshape(length, heads, -1)
    scores = jnp.einsum("ihd,jhd->hij", query_h, key_h, preferred_element_type=F32)
    scores = scores / jnp.sqrt(F32(query_h.shape[2]))
    position = jnp.arange(length)
    causal = position[:, None] >= position[None, :]
    scores = jnp.where(causal[None], scores, F32(-1e30))
    scores = scores - jnp.max(scores, axis=-1, keepdims=True)
    expo = jnp.exp(scores)
    return (expo / jnp.sum(expo, axis=-1, keepdims=True)).astype(BF)


def mm(left, right):
    return jnp.dot(left, right, preferred_element_type=F32)


def mm_nt(left, right):
    return lax.dot_general(left, right, (((1,), (1,)), ((), ())), preferred_element_type=F32)


def mm_tn(left, right):
    return lax.dot_general(left, right, (((0,), (0,)), ((), ())), preferred_element_type=F32)


def mix(probs, rows):
    heads = probs.shape[0]
    split = rows.reshape(rows.shape[0], heads, -1)
    out = jnp.einsum("hij,jhd->ihd", probs, split, preferred_element_type=F32)
    return out.reshape(out.shape[0], -1)


def mix_back(probs, rows):
    heads = probs.shape[0]
    split = rows.reshape(rows.shape[0], heads, -1)
    out = jnp.einsum("hij,ihd->jhd", probs, split, preferred_element_type=F32)
    return out.reshape(out.shape[0], -1)


def group_sum(term, count):
    term = term.astype(BF)
    if count == 1:
        return term.astype(F32)
    if count == 2:
        other = lax.ppermute(term, "tensor", ((0, 1), (1, 0)))
        return term.astype(F32) + other.astype(F32)
    share = lax.psum_scatter(term, "tensor", scatter_dimension=1, tiled=True)
    return lax.all_gather(share, "tensor", axis=1, tiled=True).astype(F32)


def full_rows(inputs, count, index):
    if count != 2:
        return lax.all_gather(inputs, "tensor", axis=1, tiled=True)
    other = lax.ppermute(inputs, "tensor", ((0, 1), (1, 0)))
    low = jnp.where(index == 0, inputs, other)
    high = jnp.where(index == 0, other, inputs)
    return jnp.concatenate([low, high], axis=1)


def gather_kernel(lines, src_ref, out_ref, own_sem, send_sem, line_sem, side_sem, core_sem):
    me = lax.axis_index("task")
    core, side, line = lax.rem(me, 2), lax.rem(me // 2, 2), me // 4

    def place(back, over_side, over_core):
        line_from = lax.rem(line + lines - back, lines)
        side_from = 1 - side if over_side else side
        core_from = 1 - core if over_core else core
        return (line_from * 2 + side_from) * 2 + core_from

    side_peer, core_peer = place(0, True, False), place(0, False, True)
    peers = [place(lines - step, False, False) for step in range(1, lines)] + [side_peer, core_peer]
    barrier = pltpu.get_barrier_semaphore()
    for peer in peers:
        pl.semaphore_signal(
            barrier, inc=1, device_id={"task": peer}, device_id_type=pl.DeviceIdType.MESH
        )
    pl.semaphore_wait(barrier, len(peers))

    started = []

    def send(source, slot, arrival, peer):
        copy = pltpu.make_async_remote_copy(
            src_ref=source,
            dst_ref=out_ref.at[slot],
            send_sem=send_sem.at[len(started)],
            recv_sem=arrival,
            device_id={"task": peer},
            device_id_type=pl.DeviceIdType.MESH,
        )
        copy.start()
        started.append(copy)

    def arrived(slot, arrival, peer):
        pltpu.make_async_remote_copy(
            src_ref=out_ref.at[slot],
            dst_ref=out_ref.at[slot],
            send_sem=send_sem.at[0],
            recv_sem=arrival,
            device_id={"task": peer},
            device_id_type=pl.DeviceIdType.MESH,
        ).wait_recv()

    for step in sorted(range(1, lines), key=lambda step: -min(step, lines - step)):
        send(src_ref, me, line_sem.at[step], peers[step - 1])
    send(src_ref, me, side_sem.at[0], side_peer)
    send(src_ref, me, core_sem.at[0, 0], core_peer)
    own = pltpu.make_async_copy(src_ref, out_ref.at[me], own_sem)
    own.start()
    order = sorted(range(1, lines), key=lambda step: min(step, lines - step))
    for step in order:
        slot = place(step, False, False)
        arrived(slot, line_sem.at[step], side_peer)
        send(out_ref.at[slot], slot, side_sem.at[step], side_peer)
        send(out_ref.at[slot], slot, core_sem.at[step, 0], core_peer)
    for step in [0] + order:
        slot = place(step, True, False)
        arrived(slot, side_sem.at[step], side_peer)
        send(out_ref.at[slot], slot, core_sem.at[step, 1], core_peer)
    for step in [0] + order:
        for over in range(2):
            arrived(place(step, over == 1, True), core_sem.at[step, over], core_peer)
    own.wait()
    for copy in started:
        copy.wait_send()


def gather_by_copies(rows, number):
    count = lax.axis_size("task")
    if count % 4:
        return gather_tokens(rows)
    lines = count // 4
    sends = (lines + 1) + 2 * (lines - 1) + lines
    gathered = pl.pallas_call(
        functools.partial(gather_kernel, lines),
        out_shape=jax.ShapeDtypeStruct((count,) + rows.shape, rows.dtype),
        in_specs=[pl.BlockSpec(memory_space=pltpu.VMEM)],
        out_specs=pl.BlockSpec(memory_space=pltpu.VMEM),
        scratch_shapes=[
            pltpu.SemaphoreType.DMA,
            pltpu.SemaphoreType.DMA((sends,)),
            pltpu.SemaphoreType.DMA((lines,)),
            pltpu.SemaphoreType.DMA((lines,)),
            pltpu.SemaphoreType.DMA((lines, 2)),
        ],
        compiler_params=pltpu.CompilerParams(collective_id=number, has_side_effects=True),
        cost_estimate=pl.CostEstimate(
            flops=0, bytes_accessed=16 * rows.size * rows.dtype.itemsize * count, transcendentals=0
        ),
    )(rows)
    return gathered.reshape(count * rows.shape[0], rows.shape[1])


def gather_tokens(rows):
    return lax.all_gather(rows, "task", axis=0, tiled=True)


def my_columns(rows):
    return lax.all_to_all(rows, "task", split_axis=1, concat_axis=0, tiled=True)


def below(rows, length):
    return jnp.pad(rows, ((0, length - rows.shape[0]), (0, 0)))


def above(rows, length):
    return jnp.pad(rows, ((length - rows.shape[0], 0), (0, 0)))


def make_device(tensor_count):
    def per_device(inputs, targets, queries, key_rows, value_weight, output_weight, splits):
        length = inputs.shape[0]
        low, high = length // 4, 3 * length // 4
        heads = queries.shape[1] // HD
        index = lax.axis_index("tensor")
        normed = normed_rows(full_rows(inputs, tensor_count, index))
        offset_here = inputs.astype(F32) - targets.astype(F32)
        offset = jnp.concatenate(
            [jnp.where(index == block, offset_here, F32(0.0)) for block in range(tensor_count)],
            axis=1,
        )
        probs = attention_probs(queries, key_rows, heads)
        probs_s = probs[:, :high, :high]
        probs_q = probs[:, low:, :]
        split = splits[0]
        count_s = split.astype(F32)
        position = jnp.arange(length)
        support = (position < split).astype(F32)[:, None]
        weight_s = (support / count_s)[:high]
        weight_q = ((1.0 - support) / (F32(length) - count_s))[low:]

        upper = mm(normed, value_weight).astype(BF)
        mixed_s = mix(probs_s, upper[:high]).astype(BF)
        gram = mm_nt(normed, normed).astype(BF)
        mixed_s_all = gather_tokens(mixed_s)
        part_0 = (mm(mixed_s, output_weight) + offset[:high]).astype(BF)
        part_0, normed_sent = lax.optimization_barrier((part_0, normed))
        normed_cols = my_columns(normed_sent)
        error_1 = (weight_s * group_sum(part_0, tensor_count)).astype(BF)

        back_u = mix_back(probs_s, mm_nt(error_1, output_weight).astype(BF)).astype(BF)
        upper_1 = (upper.astype(F32) - step_rate * mm(gram[:, :high], back_u)).astype(BF)
        mixed_q = mix(probs_q, upper_1).astype(BF)
        cross = (-step_rate * mm_nt(mixed_q, mixed_s)).astype(BF)
        part_1 = mm(mixed_q, output_weight) + mm(cross, error_1)
        part_1 = (part_1 + offset[low:]).astype(BF)
        error_2 = (weight_q * group_sum(part_1, tensor_count)).astype(BF)

        errors = (-step_rate * mm_nt(error_2, error_1)).astype(BF)
        back_z1 = (mm_nt(error_2, output_weight) + mm(errors, mixed_s)).astype(BF)
        back_u1 = mix_back(probs_q, back_z1)
        back_u1_b = back_u1.astype(BF)
        back_gram = (-step_rate * mm(gram[:high], back_u1_b)).astype(BF)
        second = mix(probs_s, back_gram).astype(BF)
        error_back = (mm(second, output_weight) + mm_tn(cross, error_2)).astype(BF)
        is_support = (position < split)[:, None]
        left = jnp.where(is_support, below(second, length), above(mixed_q, length))
        errors_both = jnp.where(is_support, below(error_1, length), above(error_2, length))
        error_back, normed_cols, errors_both, left = lax.optimization_barrier(
            (error_back, normed_cols, errors_both, left)
        )
        both_cols = my_columns(errors_both)
        left, mixed_s_all = lax.optimization_barrier((left, mixed_s_all))
        left_all = gather_tokens(left)
        error_sum = group_sum(error_back, tensor_count)
        error_3 = (weight_s * error_sum).astype(BF)
        error_3_cols = my_columns(error_3)

        back_z0 = (mm_nt(error_3, output_weight) + mm_tn(errors, mixed_q)).astype(BF)
        late = mix_back(probs_s, back_z0)
        value_rows = (back_u1 + jnp.pad(late, ((0, length - high), (0, 0)))).astype(BF)
        value_rows_all = gather_by_copies(value_rows, 1)
        total_output = (
            mm_tn(left_all, both_cols)
            + mm_tn(mixed_s_all, error_3_cols)
        )
        total_value = mm_tn(normed_cols, value_rows_all)
        return (total_value, total_output)

    return per_device


def solution(mesh):
    return jax.shard_map(
        make_device(mesh.shape["tensor"]),
        mesh=mesh,
        in_specs=(
            P("task", "tensor"),
            P("task", "tensor"),
            P("task", "tensor"),
            P("task", "tensor"),
            P(None, "tensor"),
            P("tensor", None),
            P("task"),
        ),
        out_specs=(P("task", "tensor"), P("tensor", "task")),
        check_vma=False,
    )
```

profile of v0, /device:TPU:17, one launch (start us, length us, event | category | flops | bytes accessed | tf_op | source)
XLA Modules:
  0.0 235.0 jit_solution(8156788030210971994)
XLA Ops:
  7.2 0.0 all-gather.3.cloned.1.call-start
  7.2 1.3 collective-permute-start
  9.2 1.6 fusion.64
  10.8 0.2 divide_convert_fusion
  11.1 1.4 fusion.26
  12.5 7.9 %collective-permute-done = bf16[128,2048]{1,0:T(8,128)(2,1)S(1)} collective-permute-done((bf16[128,2048]{1,0:T(8,128)(2,1)}, bf16[128,2048]{1,0:T(8,128)(2,1)S(1)}, u32[]{:S(2)}, u32[]{:S(2)}) %collective-permute-start) | collective-permute-done | bytes 524320 | tf_op jit(solution)/shard_map/ppermute | solution.py:77
  20.3 0.1 broadcast_select_fusion.1
  20.4 0.3 fusion.5
  20.7 0.3 fusion.6
  21.0 1.3 convolution_convert_fusion
  22.3 0.2 convolution_convert_fusion.3
  22.5 0.5 copy-done.10
  23.0 1.3 slice-done.1
  24.4 1.5 fusion.2
  25.9 1.3 collective-permute-start.1
  27.2 0.7 copy_bitcast_fusion.6
  28.0 0.4 convolution_convert_fusion.6
  28.4 15.2 %collective-permute-done.1 = bf16[96,4096]{1,0:T(8,128)(2,1)} collective-permute-done((bf16[96,4096]{1,0:T(8,128)(2,1)S(1)}, bf16[96,4096]{1,0:T(8,128)(2,1)}, u32[]{:S(2)}, u32[]{:S(2)}) %collective-permute-start.1) | collective-permute-done | bytes 786464 | tf_op jit(solution)/shard_map/ppermute | solution.py:68
  43.6 1.6 multiply_convert_fusion.2
  45.3 6.2 %fusion.20 = bf16[12,8,8,128]{3,2,1,0:T(8,128)(2,1)S(1)} fusion(bf16[96,4096]{1,0:T(8,128)(2,1)S(1)} %multiply_convert_fusion.2, bf16[1024,4096]{1,0:T(8,128)(2,1)} %param.12), kind=kOutput, calls=%fused_computation.44 | convolution fusion | flops 805404672 | bytes 9371648 | tf_op jit(solution)/shard_map/dot_general | solution.py:42
  51.6 0.3 fusion.17
  51.8 0.2 fusion.16
  52.1 0.2 convolution_convert_fusion.2
  52.3 1.5 fusion.63
  53.8 0.2 fusion.25
  54.1 1.3 fusion.3
  55.4 1.2 collective-permute-start.2
  56.6 0.1 slice_bitcast_fusion.2
  56.7 1.1 copy.112
  57.8 8.4 %all-to-all-start = ((bf16[128,16,256]{2,0,1:T(8,128)(2,1)}), bf16[128,16,256]{2,0,1:T(8,128)(2,1)}, u32[]{:S(2)}, u32[]{:S(2)}) async-start(bf16[128,16,256]{2,0,1:T(8,128)(2,1)} %bitcast.162), calls=%async_computation | async-start | bytes 2097152 | tf_op jit(solution)/shard_map/all_to_all | solution.py:181
  66.2 0.2 all-gather.5.cloned.1.call-start
  66.4 0.7 copy_bitcast_fusion.5
  67.1 5.3 %collective-permute-done.2 = bf16[96,4096]{1,0:T(8,128)(2,1)S(1)} collective-permute-done((bf16[96,4096]{1,0:T(8,128)(2,1)}, bf16[96,4096]{1,0:T(8,128)(2,1)S(1)}, u32[]{:S(2)}, u32[]{:S(2)}) %collective-permute-start.2) | collective-permute-done | bytes 786464 | tf_op jit(solution)/shard_map/ppermute | solution.py:68
  72.4 1.4 multiply_convert_fusion.1
  73.8 0.4 fusion.24
  74.1 0.6 copy-done.16
  74.7 0.2 fusion.61
  75.0 6.2 %fusion.22 = bf16[12,8,8,128]{3,2,1,0:T(8,128)(2,1)S(1)} fusion(f32[96,1024]{1,0:T(8,128)S(1)} %fusion.61, bf16[96,4096]{1,0:T(8,128)(2,1)S(1)} %multiply_convert_fusion.1, bf16[1024,4096]{1,0:T(8,128)(2,1)} %param.12), kind=kOutput, calls=%fused_computation.46 | convolution fusion | flops 805502976 | bytes 9764864 | tf_op jit(solution)/shard_map/dot_general | solution.py:42
  81.1 0.3 fusion.41
  81.4 0.2 copy.42
  81.6 0.9 fusion.19
  82.6 0.2 fusion.18
  82.8 0.8 pad_select_fusion.1
  83.7 4.8 %fusion.60 = f32[96,4096]{1,0:T(8,128)S(1)} fusion(bf16[1024,4096]{1,0:T(8,128)(2,1)} %param.12, bf16[8,12,8,128]{3,2,1,0:T(8,128)(2,1)S(1)} %fusion.18), kind=kOutput, calls=%fused_computation.110 | convolution fusion | flops 805306368 | bytes 10158080 | tf_op jit(solution)/shard_map/dot_general | solution.py:38
  88.5 1.3 fusion.4
  89.8 1.3 pad_select_fusion
  91.1 2.9 %all-to-all-done = bf16[128,16,256]{2,0,1:T(8,128)(2,1)} async-done(((bf16[128,16,256]{2,0,1:T(8,128)(2,1)}), bf16[128,16,256]{2,0,1:T(8,128)(2,1)}, u32[]{:S(2)}, u32[]{:S(2)}) %all-to-all-start) | async-done | bytes 1048608 | tf_op jit(solution)/shard_map/all_to_all | solution.py:181
  94.0 0.0 all-gather.5.cloned.1.call-update
  94.1 2.4 %copy.111 = bf16[16,16,8,256]{3,2,0,1:T(8,128)(2,1)} copy(bf16[16,16,8,256]{3,2,1,0:T(8,128)(2,1)} %bitcast.177) | data formatting | bytes 2097152 | tf_op jit(solution)/shard_map/all_to_all | solution.py:181
  96.4 6.0 %all-to-all-start.1 = ((bf16[128,16,256]{2,0,1:T(8,128)(2,1)}), bf16[128,16,256]{2,0,1:T(8,128)(2,1)}, u32[]{:S(2)}, u32[]{:S(2)}) async-start(bf16[128,16,256]{2,0,1:T(8,128)(2,1)} %bitcast.161), calls=%async_computation.1 | async-start | bytes 2097152 | tf_op jit(solution)/shard_map/all_to_all | solution.py:181
  102.4 1.3 collective-permute-start.3
  103.8 0.2 fusion.62
  104.0 17.3 %collective-permute-done.3 = bf16[96,4096]{1,0:T(8,128)(2,1)S(1)} collective-permute-done((bf16[96,4096]{1,0:T(8,128)(2,1)S(1)}, bf16[96,4096]{1,0:T(8,128)(2,1)S(1)}, u32[]{:S(2)}, u32[]{:S(2)}) %collective-permute-start.3) | collective-permute-done | bytes 786464 | tf_op jit(solution)/shard_map/ppermute | solution.py:68
  121.3 0.3 multiply_convert_fusion
  121.6 1.0 copy.113
  122.6 12.9 %all-to-all-done.1 = bf16[128,16,256]{2,0,1:T(8,128)(2,1)} async-done(((bf16[128,16,256]{2,0,1:T(8,128)(2,1)}), bf16[128,16,256]{2,0,1:T(8,128)(2,1)}, u32[]{:S(2)}, u32[]{:S(2)}) %all-to-all-start.1) | async-done | bytes 1048608 | tf_op jit(solution)/shard_map/all_to_all | solution.py:181
  135.5 5.1 %all-to-all-start.2 = ((bf16[96,16,256]{2,0,1:T(8,128)(2,1)}), bf16[96,16,256]{2,0,1:T(8,128)(2,1)S(1)}, u32[]{:S(2)}, u32[]{:S(2)}) async-start(bf16[96,16,256]{2,0,1:T(8,128)(2,1)} %bitcast.163), calls=%async_computation.2 | async-start | bytes 1572864 | tf_op jit(solution)/shard_map/all_to_all | solution.py:181
  140.6 6.1 %fusion.21 = bf16[12,8,8,128]{3,2,1,0:T(8,128)(2,1)S(1)} fusion(f32[96,1024]{1,0:T(8,128)S(1)} %fusion.62, bf16[96,4096]{1,0:T(8,128)(2,1)S(1)} %multiply_convert_fusion, bf16[1024,4096]{1,0:T(8,128)(2,1)} %param.12), kind=kOutput, calls=%fused_computation.45 | convolution fusion | flops 805502976 | bytes 9764864 | tf_op jit(solution)/shard_map/dot_general | solution.py:42
  146.7 0.3 convolution_bitcast_fusion
  147.0 0.8 add_convert_fusion.src_ref
  147.7 68.0 %shard_map.86 = bf16[16,128,1024]{2,1,0:T(8,128)(2,1)} custom-call(bf16[128,1024]{1,0:T(8,128)(2,1)} %add_convert_fusion.src_ref), custom_call_target="tpu_custom_call" | custom-call | bytes 67108864 | tf_op jit(solution)/shard_map/pallas_call | solution.py:156
  215.7 4.8 %fusion.69 = f32[256,1024]{1,0:T(8,128)} fusion(bf16[2048,256]{1,0:T(8,128)(2,1)} %bitcast.11, bf16[2048,1024]{1,0:T(8,128)(2,1)} %bitcast.176), kind=kOutput, calls=%fused_computation.115 | convolution fusion | flops 1073741824 | bytes 6291456 | tf_op jit(solution)/shard_map/dot_general | solution.py:46
  220.5 3.8 %fusion.70 = f32[1024,256]{1,0:T(8,128)S(1)} fusion(bf16[2048,1024]{1,0:T(8,128)(2,1)} %all-gather.5.cloned.1.call-done, bf16[2048,256]{1,0:T(8,128)(2,1)} %bitcast.16), kind=kOutput, calls=%fused_computation.116 | convolution fusion | flops 1073741824 | bytes 6291456 | tf_op jit(solution)/shard_map/dot_general | solution.py:46
  224.3 3.9 %convolution_add_fusion.3 = f32[1024,256]{1,0:T(8,128)} fusion(f32[1024,256]{1,0:T(8,128)S(1)} %fusion.70, bf16[1536,1024]{1,0:T(8,128)(2,1)} %all-gather.3.cloned.1.call-done, bf16[1536,256]{1,0:T(8,128)(2,1)S(1)} %bitcast.180), kind=kOutput, calls=%fused_computation.19 | convolution fusion | flops 805568512 | bytes 6029312 | tf_op jit(solution)/shard_map/dot_general | solution.py:46
  (55 shorter events, 0.2 us)
Async XLA Ops:
  7.2 2.0 copy-start
  7.2 3.9 %copy-start.9 = (bf16[128,2048]{1,0:T(8,128)(2,1)S(1)}, bf16[128,2048]{1,0:T(8,128)(2,1)}, u32[]{:S(2)}) copy-start(bf16[128,2048]{1,0:T(8,128)(2,1)} %param.7) | copy-start | bytes 1572868
  7.2 86.8 %all-gather.3.cloned.1.call-start = ((), (), s32[]{:S(2)}) async-start(), calls=%async_computation.3 | async-start | bytes 3342336 | tf_op jit(solution)/shard_map/all_gather | solution.py:177
  7.2 13.1 %collective-permute-start = (bf16[128,2048]{1,0:T(8,128)(2,1)}, bf16[128,2048]{1,0:T(8,128)(2,1)S(1)}, u32[]{:S(2)}, u32[]{:S(2)}) collective-permute-start(bf16[128,2048]{1,0:T(8,128)(2,1)} %param.7), channel_id=1, source_target_pairs={{0,1},{1,0},{2,3},{3,2},{4,5},{5,4},{6,7},{7,6},{8,9},{9,8},{10,11... | collective-permute-start | bytes 1572872 | tf_op jit(solution)/shard_map/ppermute | solution.py:77
  11.0 11.3 %copy-start.4 = (bf16[8,128,128]{2,1,0:T(8,128)(2,1)}, bf16[8,128,128]{2,1,0:T(8,128)(2,1)S(1)}, u32[]{:S(2)}) copy-start(bf16[8,128,128]{2,1,0:T(8,128)(2,1)S(1)} %divide_convert_fusion) | copy-start | bytes 786436
  11.1 9.9 %copy-start.1 = (bf16[4096,1024]{1,0:T(8,128)(2,1)S(1)}, bf16[4096,1024]{1,0:T(8,128)(2,1)}, u32[]{:S(2)}) copy-start(bf16[4096,1024]{1,0:T(8,128)(2,1)} %param.11) | copy-start | bytes 25165828
  12.5 10.6 %copy-start.2 = (f32[128,2048]{1,0:T(8,128)}, f32[128,2048]{1,0:T(8,128)S(1)}, u32[]{:S(2)}) copy-start(f32[128,2048]{1,0:T(8,128)S(1)} %get-tuple-element.19) | copy-start | bytes 3145732
  20.7 2.3 slice-start
  21.0 3.4 %slice-start.1 = ((s8[8388608]{0:T(1024)(128)(4,1)}), s8[4194304]{0:T(1024)(128)(4,1)S(1)}, s32[]{:S(2)}) async-start(s8[8388608]{0:T(1024)(128)(4,1)} %bitcast.170), calls=%async_computation.6 | async-start | bytes 8388608
  22.3 0.7 copy-start.10
  25.9 2.5 %copy-start.8 = (bf16[96,4096]{1,0:T(8,128)(2,1)}, bf16[96,4096]{1,0:T(8,128)(2,1)S(1)}, u32[]{:S(2)}) copy-start(bf16[96,4096]{1,0:T(8,128)(2,1)S(1)} %fusion.2) | copy-start | bytes 2359300
  25.9 17.7 %collective-permute-start.1 = (bf16[96,4096]{1,0:T(8,128)(2,1)S(1)}, bf16[96,4096]{1,0:T(8,128)(2,1)}, u32[]{:S(2)}, u32[]{:S(2)}) collective-permute-start(bf16[96,4096]{1,0:T(8,128)(2,1)S(1)} %fusion.2), channel_id=1, source_target_pairs={{0,1},{1,0},{2,3},{3,2},{4,5},{5,4},{6,7},{7,6},{8,9},{9,8},{10,11... | collective-permute-start | bytes 2359304 | tf_op jit(solution)/shard_map/ppermute | solution.py:68
  28.0 24.3 %slice-start.2 = ((s8[8388608]{0:T(1024)(128)(4,1)}), s8[4194304]{0:T(1024)(128)(4,1)S(1)}, s32[]{:S(2)}) async-start(s8[8388608]{0:T(1024)(128)(4,1)} %bitcast.172), calls=%async_computation.7 | async-start | bytes 8388608
  28.4 23.4 %copy-start.13 = (bf16[128,128]{1,0:T(8,128)(2,1)}, bf16[128,128]{1,0:T(8,128)(2,1)S(1)}, u32[]{:S(2)}) copy-start(bf16[128,128]{1,0:T(8,128)(2,1)S(1)} %convolution_convert_fusion.6) | copy-start | bytes 98308
  45.3 6.3 %copy-start.5 = (bf16[8,128,128]{2,1,0:T(8,128)(2,1)S(1)}, bf16[8,128,128]{2,1,0:T(8,128)(2,1)}, u32[]{:S(2)}) copy-start(bf16[8,128,128]{2,1,0:T(8,128)(2,1)} %copy-done.4) | copy-start | bytes 786436
  45.3 6.5 %copy-start.11 = (bf16[128,1024]{1,0:T(8,128)(2,1)S(1)}, bf16[128,1024]{1,0:T(8,128)(2,1)}, u32[]{:S(2)}) copy-start(bf16[128,1024]{1,0:T(8,128)(2,1)} %copy-done.10) | copy-start | bytes 786436
  45.3 7.0 %slice-start.3 = ((s8[8388608]{0:T(1024)(128)(4,1)}), s8[4194304]{0:T(1024)(128)(4,1)S(1)}, s32[]{:S(2)}) async-start(s8[8388608]{0:T(1024)(128)(4,1)} %bitcast.172), calls=%async_computation.8 | async-start | bytes 8388608
  52.3 1.7 copy-start.3
  54.0 1.3 copy-start.14
  55.4 17.0 %collective-permute-start.2 = (bf16[96,4096]{1,0:T(8,128)(2,1)}, bf16[96,4096]{1,0:T(8,128)(2,1)S(1)}, u32[]{:S(2)}, u32[]{:S(2)}) collective-permute-start(bf16[96,4096]{1,0:T(8,128)(2,1)} %fusion.3), channel_id=1, source_target_pairs={{0,1},{1,0},{2,3},{3,2},{4,5},{5,4},{6,7},{7,6},{8,9},{9,8},{10,11... | collective-permute-start | bytes 2359304 | tf_op jit(solution)/shard_map/ppermute | solution.py:68
  57.8 36.2 %all-to-all-start = ((bf16[128,16,256]{2,0,1:T(8,128)(2,1)}), bf16[128,16,256]{2,0,1:T(8,128)(2,1)}, u32[]{:S(2)}, u32[]{:S(2)}) async-start(bf16[128,16,256]{2,0,1:T(8,128)(2,1)} %bitcast.162), calls=%async_computation | async-start | bytes 2097152 | tf_op jit(solution)/shard_map/all_to_all | solution.py:181
  66.2 154.3 %all-gather.5.cloned.1.call-start = ((), (), s32[]{:S(2)}) async-start(), calls=%async_computation.4 | async-start | bytes 4456448 | tf_op jit(solution)/shard_map/all_gather | solution.py:177
  74.1 0.6 copy-start.16
  74.9 6.2 %copy-start.6 = (bf16[8,128,128]{2,1,0:T(8,128)(2,1)S(1)}, bf16[8,128,128]{2,1,0:T(8,128)(2,1)}, u32[]{:S(2)}) copy-start(bf16[8,128,128]{2,1,0:T(8,128)(2,1)} %copy-done.4) | copy-start | bytes 786436
  81.1 1.7 copy-start.12
  83.7 4.8 %copy-start.15 = (bf16[96,96]{1,0:T(8,128)(2,1)S(1)}, bf16[96,96]{1,0:T(8,128)(2,1)}, u32[]{:S(2)}) copy-start(bf16[96,96]{1,0:T(8,128)(2,1)} %copy-done.14) | copy-start | bytes 55300
  94.0 8.4 %copy-start.7 = (bf16[96,4096]{1,0:T(8,128)(2,1)S(1)}, bf16[96,4096]{1,0:T(8,128)(2,1)}, u32[]{:S(2)}) copy-start(bf16[96,4096]{1,0:T(8,128)(2,1)} %fusion.4) | copy-start | bytes 2359300
  94.0 9.7 %copy-start.17 = (bf16[96,96]{1,0:T(8,128)(2,1)S(1)}, bf16[96,96]{1,0:T(8,128)(2,1)}, u32[]{:S(2)}) copy-start(bf16[96,96]{1,0:T(8,128)(2,1)} %copy-done.16) | copy-start | bytes 55300
  96.4 39.1 %all-to-all-start.1 = ((bf16[128,16,256]{2,0,1:T(8,128)(2,1)}), bf16[128,16,256]{2,0,1:T(8,128)(2,1)}, u32[]{:S(2)}, u32[]{:S(2)}) async-start(bf16[128,16,256]{2,0,1:T(8,128)(2,1)} %bitcast.161), calls=%async_computation.1 | async-start | bytes 2097152 | tf_op jit(solution)/shard_map/all_to_all | solution.py:181
  102.4 18.9 %collective-permute-start.3 = (bf16[96,4096]{1,0:T(8,128)(2,1)S(1)}, bf16[96,4096]{1,0:T(8,128)(2,1)S(1)}, u32[]{:S(2)}, u32[]{:S(2)}) collective-permute-start(bf16[96,4096]{1,0:T(8,128)(2,1)S(1)} %copy-done.7), channel_id=1, source_target_pairs={{0,1},{1,0},{2,3},{3,2},{4,5},{5,4},{6,7},{7,6},{8,9},{9,8},{10,11... | collective-permute-start | bytes 2359304 | tf_op jit(solution)/shard_map/ppermute | solution.py:68
  135.5 88.8 %all-to-all-start.2 = ((bf16[96,16,256]{2,0,1:T(8,128)(2,1)}), bf16[96,16,256]{2,0,1:T(8,128)(2,1)S(1)}, u32[]{:S(2)}, u32[]{:S(2)}) async-start(bf16[96,16,256]{2,0,1:T(8,128)(2,1)} %bitcast.163), calls=%async_computation.2 | async-start | bytes 1572864 | tf_op jit(solution)/shard_map/all_to_all | solution.py:181
Sparse Core Ops, SparseCore 0:
  28.1 50.6 all-gather.2
  94.2 78.3 all-gather.4
where the time goes:
time: 236 us; the launch traced here: 235 us
  Pallas kernels  68 us (29%)
  waiting for transfers between devices  61.5 us (26%)
  matrix products  48.1 us (20%)
  starting transfers between devices  25 us (11%)
  between operations  15.3 us (6%)
  local copies, waits for them, and re-layouts  8.72 us (4%)
  other arithmetic  8.38 us (4%)
    pallas_call x1, Pallas kernels, gather_by_copies(): pl.pallas_call(functools.partial(gather_kernel, lines), out_shape=jax.Sha...  68 us
    ppermute x3, waiting for transfers between devices, group_sum(): other = lax.ppermute(term, 'tensor', ((0, 1), (1, 0)))  37.8 us
    all_to_all x3, starting transfers between devices, my_columns(): return lax.all_to_all(rows, 'task', split_axis=1, concat_axis=0, tiled=True)  19.5 us
    dot_general x6, matrix products, mm_nt(): lax.dot_general(left, right, (((1,), (1,)), ((), ())), preferred_element_...  19.5 us
    all_to_all x3, waiting for transfers between devices, my_columns(): return lax.all_to_all(rows, 'task', split_axis=1, concat_axis=0, tiled=True)  15.8 us
    dot_general x5, matrix products, mm_tn(): lax.dot_general(left, right, (((0,), (0,)), ((), ())), preferred_element_...  13.9 us
    dot_general x8, matrix products, mm(): return jnp.dot(left, right, preferred_element_type=F32)  11.8 us
    ppermute x1, waiting for transfers between devices, full_rows(): other = lax.ppermute(inputs, 'tensor', ((0, 1), (1, 0)))  7.85 us
  transfers between devices with their start and end apart: 9, of which 6 were waited for; matrix products, arithmetic and copies ran while one was open for 23% of the time, Pallas kernels for 29%

commit v1 on v0

--- a/solution.py
+++ b/solution.py
@@ -189,6 +189,458 @@
     return jnp.pad(rows, ((length - rows.shape[0], 0), (0, 0)))
 
 
+MESH = pl.DeviceIdType.MESH
+
+
+def dot_of(left, right, dims):
+    return lax.dot_general(left, right, (dims, ((), ())), preferred_element_type=F32)
+
+
+def step_kernel(
+    lines,
+    x_in, t_in, q_in, k_in, v_in, o_in, split_ref,
+    dv_ref, do_ref,
+    xf, tg, qs, ks, vw, ow, probs, probs_t, upper, mixq, second, acc, half_acc,
+    part_0, part_1, part_2, got_0, got_1, got_2, err_1, err_2, err_3, both,
+    back, gram_b, cross, pairs, value_now, z_all, left_all, rows_all, x_cols, both_cols, err_cols,
+    load_sem, x_sem, part_sem, part_got,
+    a2a_send, a2a_got, g_send, g_line, g_side, g_core,
+):
+    count = lines * 4
+    length, depth = xf.shape
+    half = depth // 2
+    width = upper.shape[1]
+    heads = width // HD
+    low, high = length // 4, 3 * length // 4
+    piece = depth // count
+    chunks = 8
+    cut = depth // chunks
+    near = chunks // 2
+
+    me = lax.axis_index("task")
+    mine = lax.axis_index("tensor")
+    core, side, line = lax.rem(me, 2), lax.rem(me // 2, 2), me // 4
+    pair = {"tensor": 1 - mine}
+
+    def place(back_by, over_side, over_core):
+        line_from = lax.rem(line + lines - back_by, lines)
+        side_from = 1 - side if over_side else side
+        core_from = 1 - core if over_core else core
+        return (line_from * 2 + side_from) * 2 + core_from
+
+    def lanes(start, size):
+        return pl.ds(pl.multiple_of(start, 128), size)
+
+    own_half = lanes(mine * half, half)
+    loads = [
+        pltpu.make_async_copy(x_in, xf.at[:, own_half], load_sem.at[0]),
+        pltpu.make_async_copy(q_in, qs, load_sem.at[1]),
+        pltpu.make_async_copy(k_in, ks, load_sem.at[2]),
+        pltpu.make_async_copy(v_in, vw, load_sem.at[3]),
+        pltpu.make_async_copy(t_in, tg, load_sem.at[4]),
+        pltpu.make_async_copy(o_in, ow, load_sem.at[5]),
+    ]
+    for load in loads:
+        load.start()
+
+    barrier = pltpu.get_barrier_semaphore()
+    for step in range(1, count):
+        pl.semaphore_signal(
+            barrier, inc=1, device_id={"task": lax.rem(me + step, count)}, device_id_type=MESH
+        )
+    pl.semaphore_signal(barrier, inc=1, device_id=pair, device_id_type=MESH)
+    pl.semaphore_wait(barrier, count)
+
+    def remote(src, dst, send, got, peer):
+        return pltpu.make_async_remote_copy(
+            src_ref=src, dst_ref=dst, send_sem=send, recv_sem=got, device_id=peer, device_id_type=MESH
+        )
+
+    def x_copy(k, owner):
+        part = xf.at[:, lanes(owner * half + k * cut, cut)]
+        return remote(part, part, x_sem.at[0, k], x_sem.at[1, k], pair)
+
+    loads[0].wait()
+    for k in range(near):
+        x_copy(k, mine).start()
+
+    def a2a_copy(number, src, dst, step):
+        peer = lax.rem(me + step, count)
+        return remote(
+            src.at[:, lanes(peer * piece, piece)],
+            dst.at[me],
+            a2a_send.at[number, step],
+            a2a_got.at[number, step],
+            {"task": peer},
+        )
+
+    def a2a_start(number, src, dst):
+        def one(step, carry):
+            a2a_copy(number, src, dst, step).start()
+            return carry
+        lax.fori_loop(1, count, one, 0)
+
+    def a2a_wait(number, src, dst):
+        def one(step, carry):
+            a2a_copy(number, src, dst, step).wait()
+            return carry
+        lax.fori_loop(1, count, one, 0)
+
+    def x_spread(own):
+        def one(step, carry):
+            peer = lax.rem(me + step, count)
+            here = (peer // (count // 2)) == mine
+            @pl.when(here if own else jnp.logical_not(here))
+            def _():
+                a2a_copy(0, xf, x_cols, step).start()
+            return carry
+        lax.fori_loop(1, count, one, 0)
+
+    x_spread(True)
+
+    def gather_copy(number, src, dst, peer, index, got):
+        return remote(src, dst, g_send.at[number, index], got, {"task": peer})
+
+    def gather_start(number, array):
+        src = array.at[me]
+        index = 0
+        for step in range(1, lines):
+            gather_copy(number, src, src, place(lines - step, False, False), index, g_line.at[number, step]).start()
+            index += 1
+        gather_copy(number, src, src, place(0, True, False), index, g_side.at[number, 0]).start()
+        gather_copy(number, src, src, place(0, False, True), index + 1, g_core.at[number, 0, 0]).start()
+
+    def gather_relay_line(number, array):
+        index = lines + 1
+        for step in range(1, lines):
+            slot = array.at[place(step, False, False)]
+            gather_copy(number, slot, slot, place(0, True, False), index, g_line.at[number, step]).wait_recv()
+            gather_copy(number, slot, slot, place(0, True, False), index, g_side.at[number, step]).start()
+            gather_copy(number, slot, slot, place(0, False, True), index + 1, g_core.at[number, step, 0]).start()
+            index += 2
+
+    def gather_relay_side(number, array):
+        index = lines + 1 + 2 * (lines - 1)
+        for step in range(lines):
+            slot = array.at[place(step, True, False)]
+            gather_copy(number, slot, slot, place(0, False, True), index, g_side.at[number, step]).wait_recv()
+            gather_copy(number, slot, slot, place(0, False, True), index, g_core.at[number, step, 1]).start()
+            index += 1
+
+    def gather_finish(number, array):
+        for step in range(lines):
+            for over in range(2):
+                slot = array.at[place(step, over == 1, True)]
+                gather_copy(number, slot, slot, place(0, False, True), 0, g_core.at[number, step, over]).wait_recv()
+
+    def gather_sent(number, array):
+        for index in range(lines + 1 + 2 * (lines - 1) + lines):
+            gather_copy(number, array.at[me], array.at[me], place(0, False, True), index, g_core.at[number, 0, 0]).wait_send()
+
+    def head(h):
+        return slice(h * HD, (h + 1) * HD)
+
+    row = lax.broadcasted_iota(jnp.int32, (length, length), 0)
+    col = lax.broadcasted_iota(jnp.int32, (length, length), 1)
+    causal = row >= col
+    loads[1].wait()
+    loads[2].wait()
+    root = jnp.sqrt(F32(HD))
+    for h in range(heads):
+        scores = dot_of(qs[:, head(h)], ks[:, head(h)], ((1,), (1,))) / root
+        scores = jnp.where(causal, scores, F32(-1e30))
+        scores = scores - jnp.max(scores, axis=-1, keepdims=True)
+        expo = jnp.exp(scores)
+        prob = expo / jnp.sum(expo, axis=-1, keepdims=True)
+        probs[:, head(h)] = prob.astype(BF)
+        probs_t[:, head(h)] = prob.T.astype(BF)
+
+    err_1[high:, :] = jnp.zeros((length - high, depth), BF)
+    err_2[:low, :] = jnp.zeros((low, depth), BF)
+    err_3[high:, :] = jnp.zeros((length - high, depth), BF)
+    position = lax.broadcasted_iota(jnp.int32, (length, 1), 0)
+    split = jnp.full((length, 1), split_ref[0], jnp.int32)
+    is_support = position < split
+    support = is_support.astype(F32)
+    count_s = split.astype(F32)
+    weight_s = support / count_s
+    weight_q = (1.0 - support) / (F32(length) - count_s)
+
+    loads[3].wait()
+
+    def take(k, owner, first):
+        at = lanes(owner * half + k * cut, cut)
+        x_part = xf[:, at]
+        new = dot_of(x_part, vw[pl.ds(pl.multiple_of(owner * half + k * cut, 128), cut), :], ((1,), (0,)))
+        gram = dot_of(x_part, x_part, ((1,), (1,)))
+        if first:
+            acc[...] = new
+            half_acc[...] = gram
+        else:
+            acc[...] += new
+            half_acc[...] += gram
+
+    take(0, mine, True)
+    def own_take(k, carry):
+        take(k, mine, False)
+        return carry
+    lax.fori_loop(1, near, own_take, 0)
+    def other_take(k, carry):
+        x_copy(k, 1 - mine).wait_recv()
+        take(k, 1 - mine, False)
+        return carry
+    lax.fori_loop(0, near, other_take, 0)
+    x_spread(False)
+
+    gram_raw = half_acc[...]
+    diagonal = jnp.where(row == col, gram_raw, F32(0.0))
+    scale_row = lax.rsqrt(jnp.sum(diagonal, axis=1, keepdims=True) / F32(depth) + 1e-05)
+    scale_col = lax.rsqrt(jnp.sum(diagonal, axis=0, keepdims=True) / F32(depth) + 1e-05)
+    gram_b[...] = (gram_raw * scale_row * scale_col).astype(BF)
+    upper[...] = (acc[...] * scale_row).astype(BF)
+
+    z_mine = z_all.at[me]
+    for h in range(heads):
+        mixed = dot_of(probs[:, head(h)], upper[:, head(h)], ((1,), (0,)))
+        z_mine[:, head(h)] = mixed[:high].astype(BF)
+    loads[4].wait()
+    loads[5].wait()
+
+    def part_copy(number, send, got, k, owner):
+        at = lanes(lax.rem(owner * near + k, chunks) * cut, cut)
+        return remote(send.at[:, at], got.at[:, at], part_sem.at[number, k], part_got.at[number, k], pair)
+
+    def own_columns(k):
+        return lanes(lax.rem(mine * near + k, chunks) * cut, cut)
+
+    def other_columns(k):
+        return lanes(lax.rem((1 - mine) * near + k, chunks) * cut, cut)
+
+    def offset(k, rows):
+        there = lanes(k * cut, cut)
+        return xf[rows, own_columns(k)].astype(F32) - tg[rows, there].astype(F32)
+
+    def send_parts(number, value, rows, send, got, with_offset):
+        def one(k, near_half):
+            at = own_columns(k)
+            part = value(at)
+            if near_half and with_offset:
+                part = part + offset(k, rows)
+            send[:, at] = part.astype(BF)
+            part_copy(number, send, got, k, mine).start()
+        def first(k, carry):
+            one(k, True)
+            return carry
+        def later(k, carry):
+            one(k, False)
+            return carry
+        lax.fori_loop(0, near, first, 0)
+        lax.fori_loop(near, chunks, later, 0)
+
+    def take_parts(number, send, got, rows, weight, error, also):
+        def one(k, carry):
+            at = other_columns(k)
+            part_copy(number, send, got, k, 1 - mine).wait_recv()
+            total = send[:, at].astype(F32) + got[:, at].astype(F32)
+            error[rows, at] = (weight[rows] * total).astype(BF)
+            part = error[:, at]
+            acc[...] += dot_of(part, ow[:, at], ((1,), (1,)))
+            also(at, part)
+            return carry
+        lax.fori_loop(0, chunks, one, 0)
+
+    support_rows, query_rows = slice(0, high), slice(low, length)
+    nothing = lambda at, part: None
+
+    def value_0(at):
+        return dot_of(z_mine[...], ow[:, at], ((1,), (0,)))
+
+    acc[...] = jnp.zeros_like(acc)
+    send_parts(0, value_0, support_rows, part_0, got_0, True)
+    gather_start(0, z_all)
+    take_parts(0, part_0, got_0, support_rows, weight_s, err_1, nothing)
+
+    back[...] = acc[...].astype(BF)
+    for h in range(heads):
+        up = dot_of(probs_t[:, head(h)], back[:, head(h)], ((1,), (0,))).astype(BF)
+        new = (upper[:, head(h)].astype(F32) - step_rate * dot_of(gram_b[...], up, ((1,), (0,)))).astype(BF)
+        mixq[:, head(h)] = dot_of(probs[:, head(h)], new, ((1,), (0,))).astype(BF)
+    cross[:, :high] = (-step_rate * dot_of(mixq[...], z_mine[...], ((1,), (1,)))).astype(BF)
+
+    def value_1(at):
+        part = dot_of(mixq[...], ow[:, at], ((1,), (0,))) + dot_of(cross[:, :high], err_1[:high, at], ((1,), (0,)))
+        return part[low:]
+
+    half_acc[...] = jnp.zeros_like(half_acc)
+    acc[...] = jnp.zeros_like(acc)
+
+    def pairs_of(at, part):
+        half_acc[...] += dot_of(part, err_1[:, at], ((1,), (1,)))
+
+    send_parts(1, value_1, query_rows, part_1, got_1, True)
+    gather_relay_line(0, z_all)
+    take_parts(1, part_1, got_1, query_rows, weight_q, err_2, pairs_of)
+    gather_relay_side(0, z_all)
+
+    pairs[...] = (-step_rate * half_acc[...]).astype(BF)
+    back[...] = (acc[...] + dot_of(pairs[:, :high], z_mine[...], ((1,), (0,)))).astype(BF)
+    left_mine = left_all.at[me]
+    for h in range(heads):
+        up = dot_of(probs_t[:, head(h)], back[:, head(h)], ((1,), (0,)))
+        value_now[:, head(h)] = up
+        flow = (-step_rate * dot_of(gram_b[...], up.astype(BF), ((1,), (0,)))).astype(BF)
+        again = dot_of(probs[:, head(h)], flow, ((1,), (0,))).astype(BF)
+        second[:, head(h)] = again
+        left_mine[:, head(h)] = jnp.where(is_support, again, mixq[:, head(h)])
+
+    def value_2(at):
+        part = dot_of(second[...], ow[:, at], ((1,), (0,))) + dot_of(cross[...], err_2[:, at], ((0,), (0,)))
+        return part[:high]
+
+    acc[...] = jnp.zeros_like(acc)
+    cross[:, high:] = jnp.zeros((length, length - high), BF)
+    send_parts(2, value_2, support_rows, part_2, got_2, False)
+
+    def join(k, carry):
+        at = own_columns(k)
+        both[:, at] = jnp.where(is_support, err_1[:, at], err_2[:, at])
+        return carry
+    lax.fori_loop(0, chunks, join, 0)
+    a2a_start(1, both, both_cols)
+    gather_start(1, left_all)
+    take_parts(2, part_2, got_2, support_rows, weight_s, err_3, nothing)
+    a2a_start(2, err_3.at[:high], err_cols)
+
+    back[...] = (acc[...] + dot_of(pairs[...], mixq[...], ((0,), (0,)))).astype(BF)
+    rows_mine = rows_all.at[me]
+    for h in range(heads):
+        late = dot_of(probs_t[:, head(h)], back[:, head(h)], ((1,), (0,)))
+        rows_mine[:, head(h)] = ((value_now[:, head(h)] + late) * scale_row).astype(BF)
+    gather_relay_line(1, left_all)
+    gather_start(2, rows_all)
+    gather_relay_side(1, left_all)
+
+    x_cols[me] = xf[:, lanes(me * piece, piece)]
+    both_cols[me] = both[:, lanes(me * piece, piece)]
+    err_cols[me] = err_3[:high, lanes(me * piece, piece)]
+
+    a2a_wait(0, xf, x_cols)
+    a2a_wait(1, both, both_cols)
+    gather_finish(0, z_all)
+    gather_relay_line(2, rows_all)
+    gather_finish(1, left_all)
+
+    tile = 256
+
+    def early(i, carry):
+        at = lanes(i * tile, tile)
+        do_ref[at, :] = dot_of(
+            left_all[:, :, at].reshape(count * length, tile), both_cols[...].reshape(count * length, piece), ((0,), (0,))
+        )
+        return carry
+    lax.fori_loop(0, width // tile, early, 0)
+    gather_relay_side(2, rows_all)
+    a2a_wait(2, err_3.at[:high], err_cols)
+
+    def late_part(i, carry):
+        at = lanes(i * tile, tile)
+        do_ref[at, :] += dot_of(
+            z_all[:, :, at].reshape(count * high, tile), err_cols[...].reshape(count * high, piece), ((0,), (0,))
+        )
+        return carry
+    lax.fori_loop(0, width // tile, late_part, 0)
+    gather_finish(2, rows_all)
+
+    def last(i, carry):
+        at = lanes(i * tile, tile)
+        dv_ref[:, at] = dot_of(
+            x_cols[...].reshape(count * length, piece), rows_all[:, :, at].reshape(count * length, tile), ((0,), (0,))
+        )
+        return carry
+    lax.fori_loop(0, width // tile, last, 0)
+
+    for k in range(near):
+        x_copy(k, mine).wait_send()
+    for number, (send, got) in enumerate(((part_0, got_0), (part_1, got_1), (part_2, got_2))):
+        for k in range(chunks):
+            part_copy(number, send, got, k, mine).wait_send()
+    for number, array in enumerate((z_all, left_all, rows_all)):
+        gather_sent(number, array)
+
+
+def one_kernel(inputs, targets, queries, key_rows, value_weight, output_weight, splits):
+    count = lax.axis_size("task")
+    lines = count // 4
+    length, half = inputs.shape
+    depth = 2 * half
+    width = queries.shape[1]
+    high = 3 * length // 4
+    piece = depth // count
+    sends = (lines + 1) + 2 * (lines - 1) + lines
+    vm = pltpu.VMEM
+    dma = pltpu.SemaphoreType.DMA
+    anywhere = pl.BlockSpec(memory_space=pl.ANY)
+    chunks = 8
+    return pl.pallas_call(
+        functools.partial(step_kernel, lines),
+        out_shape=(
+            jax.ShapeDtypeStruct((piece, width), F32),
+            jax.ShapeDtypeStruct((width, piece), F32),
+        ),
+        in_specs=[anywhere] * 6 + [pl.BlockSpec(memory_space=pltpu.SMEM)],
+        out_specs=(pl.BlockSpec(memory_space=pltpu.VMEM), pl.BlockSpec(memory_space=pltpu.VMEM)),
+        scratch_shapes=[
+            vm((length, depth), BF),
+            vm((length, half), BF),
+            vm((length, width), BF),
+            vm((length, width), BF),
+            vm((depth, width), BF),
+            vm((width, depth), BF),
+            vm((length, width), BF),
+            vm((length, width), BF),
+            vm((length, width), BF),
+            vm((length, width), BF),
+            vm((length, width), BF),
+            vm((length, width), F32),
+            vm((length, length), F32),
+            vm((high, depth), BF),
+            vm((high, depth), BF),
+            vm((high, depth), BF),
+            vm((high, depth), BF),
+            vm((high, depth), BF),
+            vm((high, depth), BF),
+            vm((length, depth), BF),
+            vm((length, depth), BF),
+            vm((length, depth), BF),
+            vm((length, depth), BF),
+            vm((length, width), BF),
+            vm((length, length), BF),
+            vm((length, length), BF),
+            vm((length, length), BF),
+            vm((length, width), F32),
+            vm((count, high, width), BF),
+            vm((count, length, width), BF),
+            vm((count, length, width), BF),
+            vm((count, length, piece), BF),
+            vm((count, length, piece), BF),
+            vm((count, high, piece), BF),
+            dma((6,)),
+            dma((2, chunks // 2)),
+            dma((3, chunks)),
+            dma((3, chunks)),
+            dma((3, count)),
+            dma((3, count)),
+            dma((3, sends)),
+            dma((3, lines)),
+            dma((3, lines)),
+            dma((3, lines, 2)),
+        ],
+        compiler_params=pltpu.CompilerParams(
+            collective_id=1, has_side_effects=True, vmem_limit_bytes=60 * 2**20
+        ),
+    )(inputs, targets, queries, key_rows, value_weight, output_weight, splits)
+
+
 def make_device(tensor_count):
     def per_device(inputs, targets, queries, key_rows, value_weight, output_weight, splits):
         length = inputs.shape[0]
@@ -263,8 +715,9 @@
 
 
 def solution(mesh):
+    whole_step = mesh.shape["tensor"] == 2 and mesh.shape["task"] % 4 == 0
     return jax.shard_map(
-        make_device(mesh.shape["tensor"]),
+        one_kernel if whole_step else make_device(mesh.shape["tensor"]),
         mesh=mesh,
         in_specs=(
             P("task", "tensor"),

time: 236 us -> 189 us (0.80)
  the two profiles are of different devices: /device:TPU:17 before, /device:TPU:18 now
where the time goes in v1:
time: 189 us
  Pallas kernels  183 us (97%)
  local copies, waits for them, and re-layouts  4.57 us (2%)
    pallas_call x1, Pallas kernels, one_kernel(): pl.pallas_call(functools.partial(step_kernel, lines), out_shape=(jax.Shap...  183 us
    unnamed x2, local copies, waits for them, and re-layouts  4.57 us

profile of v1, /device:TPU:18, one launch (start us, length us, event | category | flops | bytes accessed | tf_op | source)
XLA Modules:
  0.0 189.2 jit_solution(17337087690041086056)
XLA Ops:
  1.3 183.3 %shard_map.86 = (f32[256,1024]{1,0:T(8,128)}, f32[1024,256]{1,0:T(8,128)}) custom-call(bf16[128,2048]{1,0:T(8,128)(2,1)} %x_in.1, bf16[128,2048]{1,0:T(8,128)(2,1)} %t_in.1, bf16[128,1024]{1,0:T(8,128)(2,1)} %q_in.1, bf16[128,1024]{1,0:T(8,128)(2,1)} %k_in.1, bf16[4096,1024]{1,0:T(8,128)(2,1)} %v_in.1, bf16[1024,4096]{1,0:T(8,128)(2,1)} %o_in.1, ...), custom_call_target="tpu_custom_call" | custom-call | tf_op jit(solution)/shard_map/pallas_call | solution.py:584
  184.6 2.3 %copy.12 = f32[256,1024]{1,0:T(8,128)} copy(f32[256,1024]{1,0:T(8,128)} %get-tuple-element.4) | data formatting | bytes 2097152
  186.9 2.3 %copy.13 = f32[1024,256]{1,0:T(8,128)} copy(f32[1024,256]{1,0:T(8,128)} %get-tuple-element.5) | data formatting | bytes 2097152

commit v2 on v1

--- a/solution.py
+++ b/solution.py
@@ -200,10 +200,11 @@
     lines,
     x_in, t_in, q_in, k_in, v_in, o_in, split_ref,
     dv_ref, do_ref,
-    xf, tg, qs, ks, vw, ow, probs, probs_t, upper, mixq, second, acc, half_acc,
+    xf, tg, qs, ks, vw, ow, probs, probs_t, upper, mixq, second, left, acc, half_acc,
     part_0, part_1, part_2, got_0, got_1, got_2, err_1, err_2, err_3, both,
-    back, gram_b, cross, pairs, value_now, z_all, left_all, rows_all, x_cols, both_cols, err_cols,
-    load_sem, x_sem, part_sem, part_got,
+    back, gram_b, cross, cross_got, pairs, value_now, z_mine, a_all, left_all, rows_all,
+    x_cols, both_cols, right_a, swap, swap_got,
+    load_sem, x_sem, part_sem, part_got, cross_sem, swap_sem,
     a2a_send, a2a_got, g_send, g_line, g_side, g_core,
 ):
     count = lines * 4
@@ -222,11 +223,8 @@
     core, side, line = lax.rem(me, 2), lax.rem(me // 2, 2), me // 4
     pair = {"tensor": 1 - mine}
 
-    def place(back_by, over_side, over_core):
-        line_from = lax.rem(line + lines - back_by, lines)
-        side_from = 1 - side if over_side else side
-        core_from = 1 - core if over_core else core
-        return (line_from * 2 + side_from) * 2 + core_from
+    def place(line_at, side_at, core_at):
+        return (line_at * 2 + side_at) * 2 + core_at
 
     def lanes(start, size):
         return pl.ds(pl.multiple_of(start, 128), size)
@@ -264,27 +262,29 @@
     for k in range(near):
         x_copy(k, mine).start()
 
-    def a2a_copy(number, src, dst, step):
+    def a2a_copy(number, src, dst, rows, step):
         peer = lax.rem(me + step, count)
         return remote(
-            src.at[:, lanes(peer * piece, piece)],
-            dst.at[me],
+            src.at[rows, lanes(peer * piece, piece)],
+            dst.at[me, rows],
             a2a_send.at[number, step],
             a2a_got.at[number, step],
             {"task": peer},
         )
 
-    def a2a_start(number, src, dst):
+    def a2a_start(number, src, dst, rows, first=1, last=count):
         def one(step, carry):
-            a2a_copy(number, src, dst, step).start()
+            a2a_copy(number, src, dst, rows, step).start()
+            return carry
+        lax.fori_loop(first, last, one, 0)
+
+    def a2a_wait(number, src, dst, rows):
+        def one(step, carry):
+            a2a_copy(number, src, dst, rows, step).wait()
             return carry
         lax.fori_loop(1, count, one, 0)
 
-    def a2a_wait(number, src, dst):
-        def one(step, carry):
-            a2a_copy(number, src, dst, step).wait()
-            return carry
-        lax.fori_loop(1, count, one, 0)
+    all_rows = pl.ds(0, length)
 
     def x_spread(own):
         def one(step, carry):
@@ -292,50 +292,69 @@
             here = (peer // (count // 2)) == mine
             @pl.when(here if own else jnp.logical_not(here))
             def _():
-                a2a_copy(0, xf, x_cols, step).start()
+                a2a_copy(0, xf, x_cols, all_rows, step).start()
             return carry
         lax.fori_loop(1, count, one, 0)
 
     x_spread(True)
 
-    def gather_copy(number, src, dst, peer, index, got):
-        return remote(src, dst, g_send.at[number, index], got, {"task": peer})
+    def gather_copy(number, array, slot, kind, source, got, peer):
+        block = array.at[slot]
+        return remote(block, block, g_send.at[number, kind, source], got, {"task": peer})
+
+    up_peer, down_peer = me + 4, me - 4
+    side_peer, core_peer = place(line, 1 - side, core), place(line, side, 1 - core)
+
+    def pass_on(number, array, source):
+        slot = place(source, side, core)
+        @pl.when(jnp.logical_and(source <= line, line < lines - 1))
+        def _():
+            gather_copy(number, array, slot, 0, source, g_line.at[number, source], up_peer).start()
+        @pl.when(jnp.logical_and(source >= line, line > 0))
+        def _():
+            gather_copy(number, array, slot, 1, source, g_line.at[number, source], down_peer).start()
+        gather_copy(number, array, slot, 2, source, g_side.at[number, source], side_peer).start()
+        gather_copy(number, array, slot, 3, source, g_core.at[number, source, 0], core_peer).start()
 
     def gather_start(number, array):
-        src = array.at[me]
-        index = 0
-        for step in range(1, lines):
-            gather_copy(number, src, src, place(lines - step, False, False), index, g_line.at[number, step]).start()
-            index += 1
-        gather_copy(number, src, src, place(0, True, False), index, g_side.at[number, 0]).start()
-        gather_copy(number, src, src, place(0, False, True), index + 1, g_core.at[number, 0, 0]).start()
-
-    def gather_relay_line(number, array):
-        index = lines + 1
-        for step in range(1, lines):
-            slot = array.at[place(step, False, False)]
-            gather_copy(number, slot, slot, place(0, True, False), index, g_line.at[number, step]).wait_recv()
-            gather_copy(number, slot, slot, place(0, True, False), index, g_side.at[number, step]).start()
-            gather_copy(number, slot, slot, place(0, False, True), index + 1, g_core.at[number, step, 0]).start()
-            index += 2
-
-    def gather_relay_side(number, array):
-        index = lines + 1 + 2 * (lines - 1)
-        for step in range(lines):
-            slot = array.at[place(step, True, False)]
-            gather_copy(number, slot, slot, place(0, False, True), index, g_side.at[number, step]).wait_recv()
-            gather_copy(number, slot, slot, place(0, False, True), index, g_core.at[number, step, 1]).start()
-            index += 1
+        pass_on(number, array, line)
+
+    def gather_line(number, array, away):
+        def take(source):
+            slot = place(source, side, core)
+            gather_copy(number, array, slot, 2, source, g_line.at[number, source], side_peer).wait_recv()
+            pass_on(number, array, source)
+        @pl.when(line >= away)
+        def _():
+            take(line - away)
+        @pl.when(line + away < lines)
+        def _():
+            take(line + away)
+
+    def gather_side(number, array):
+        for source in range(lines):
+            slot = place(source, 1 - side, core)
+            gather_copy(number, array, slot, 4, source, g_side.at[number, source], core_peer).wait_recv()
+            gather_copy(number, array, slot, 4, source, g_core.at[number, source, 1], core_peer).start()
 
     def gather_finish(number, array):
-        for step in range(lines):
+        for source in range(lines):
             for over in range(2):
-                slot = array.at[place(step, over == 1, True)]
-                gather_copy(number, slot, slot, place(0, False, True), 0, g_core.at[number, step, over]).wait_recv()
+                slot = place(source, side if over == 0 else 1 - side, 1 - core)
+                gather_copy(number, array, slot, 3, source, g_core.at[number, source, over], core_peer).wait_recv()
 
     def gather_sent(number, array):
-        for index in range(lines + 1 + 2 * (lines - 1) + lines):
-            gather_copy(number, array.at[me], array.at[me], place(0, False, True), index, g_core.at[number, 0, 0]).wait_send()
+        def sent(kind, source):
+            gather_copy(number, array, me, kind, source, g_core.at[number, source, 0], core_peer).wait_send()
+        for source in range(lines):
+            @pl.when(jnp.logical_and(source <= line, line < lines - 1))
+            def _():
+                sent(0, source)
+            @pl.when(jnp.logical_and(source >= line, line > 0))
+            def _():
+                sent(1, source)
+            for kind in range(2, 5):
+                sent(kind, source)
 
     def head(h):
         return slice(h * HD, (h + 1) * HD)
@@ -399,10 +418,11 @@
     gram_b[...] = (gram_raw * scale_row * scale_col).astype(BF)
     upper[...] = (acc[...] * scale_row).astype(BF)
 
-    z_mine = z_all.at[me]
+    a_mine = a_all.at[me]
     for h in range(heads):
         mixed = dot_of(probs[:, head(h)], upper[:, head(h)], ((1,), (0,)))
         z_mine[:, head(h)] = mixed[:high].astype(BF)
+    a_mine[:high, :] = (weight_s[:high] * z_mine[...].astype(F32)).astype(BF)
     loads[4].wait()
     loads[5].wait()
 
@@ -437,7 +457,7 @@
         lax.fori_loop(0, near, first, 0)
         lax.fori_loop(near, chunks, later, 0)
 
-    def take_parts(number, send, got, rows, weight, error, also):
+    def take_parts(number, send, got, rows, weight, error, also, first=0, last=chunks):
         def one(k, carry):
             at = other_columns(k)
             part_copy(number, send, got, k, 1 - mine).wait_recv()
@@ -447,7 +467,7 @@
             acc[...] += dot_of(part, ow[:, at], ((1,), (1,)))
             also(at, part)
             return carry
-        lax.fori_loop(0, chunks, one, 0)
+        lax.fori_loop(first, last, one, 0)
 
     support_rows, query_rows = slice(0, high), slice(low, length)
     nothing = lambda at, part: None
@@ -455,17 +475,22 @@
     def value_0(at):
         return dot_of(z_mine[...], ow[:, at], ((1,), (0,)))
 
+    early_rows, middle_rows, late_rows = pl.ds(0, low), pl.ds(low, high - low), pl.ds(high, length - high)
     acc[...] = jnp.zeros_like(acc)
     send_parts(0, value_0, support_rows, part_0, got_0, True)
-    gather_start(0, z_all)
     take_parts(0, part_0, got_0, support_rows, weight_s, err_1, nothing)
+    a2a_start(1, err_1, both_cols, early_rows)
 
     back[...] = acc[...].astype(BF)
     for h in range(heads):
         up = dot_of(probs_t[:, head(h)], back[:, head(h)], ((1,), (0,))).astype(BF)
         new = (upper[:, head(h)].astype(F32) - step_rate * dot_of(gram_b[...], up, ((1,), (0,)))).astype(BF)
         mixq[:, head(h)] = dot_of(probs[:, head(h)], new, ((1,), (0,))).astype(BF)
-    cross[:, :high] = (-step_rate * dot_of(mixq[...], z_mine[...], ((1,), (1,)))).astype(BF)
+    cross[:, high:] = jnp.zeros((length, length - high), BF)
+    product = -step_rate * dot_of(mixq[...], z_mine[...], ((1,), (1,)))
+    cross[:, :high] = jnp.where(is_support, F32(0.0), product).astype(BF)
+    cross_copy = remote(cross, cross_got, cross_sem.at[0], cross_sem.at[1], pair)
+    cross_copy.start()
 
     def value_1(at):
         part = dot_of(mixq[...], ow[:, at], ((1,), (0,))) + dot_of(cross[:, :high], err_1[:high, at], ((1,), (0,)))
@@ -478,9 +503,14 @@
         half_acc[...] += dot_of(part, err_1[:, at], ((1,), (1,)))
 
     send_parts(1, value_1, query_rows, part_1, got_1, True)
-    gather_relay_line(0, z_all)
-    take_parts(1, part_1, got_1, query_rows, weight_q, err_2, pairs_of)
-    gather_relay_side(0, z_all)
+    cross_copy.wait_recv()
+    cross_sum = (cross[...].astype(F32) + cross_got[...].astype(F32)).astype(BF)
+    left[...] = (mixq[...].astype(F32) + dot_of(cross_sum[:, :high], a_mine[:high], ((1,), (0,)))).astype(BF)
+    a_mine[high:, :] = left[high:, :]
+    gather_start(0, a_all)
+    take_parts(1, part_1, got_1, query_rows, weight_q, err_2, pairs_of, 0, 5)
+    gather_line(0, a_all, 1)
+    take_parts(1, part_1, got_1, query_rows, weight_q, err_2, pairs_of, 5, chunks)
 
     pairs[...] = (-step_rate * half_acc[...]).astype(BF)
     back[...] = (acc[...] + dot_of(pairs[:, :high], z_mine[...], ((1,), (0,)))).astype(BF)
@@ -491,14 +521,14 @@
         flow = (-step_rate * dot_of(gram_b[...], up.astype(BF), ((1,), (0,)))).astype(BF)
         again = dot_of(probs[:, head(h)], flow, ((1,), (0,))).astype(BF)
         second[:, head(h)] = again
-        left_mine[:, head(h)] = jnp.where(is_support, again, mixq[:, head(h)])
+        left_mine[:, head(h)] = jnp.where(is_support, again, left[:, head(h)])[:high]
 
     def value_2(at):
         part = dot_of(second[...], ow[:, at], ((1,), (0,))) + dot_of(cross[...], err_2[:, at], ((0,), (0,)))
         return part[:high]
 
     acc[...] = jnp.zeros_like(acc)
-    cross[:, high:] = jnp.zeros((length, length - high), BF)
+    gather_start(1, left_all)
     send_parts(2, value_2, support_rows, part_2, got_2, False)
 
     def join(k, carry):
@@ -506,46 +536,83 @@
         both[:, at] = jnp.where(is_support, err_1[:, at], err_2[:, at])
         return carry
     lax.fori_loop(0, chunks, join, 0)
-    a2a_start(1, both, both_cols)
-    gather_start(1, left_all)
-    take_parts(2, part_2, got_2, support_rows, weight_s, err_3, nothing)
-    a2a_start(2, err_3.at[:high], err_cols)
+    gather_line(0, a_all, 2)
+    take_parts(2, part_2, got_2, support_rows, weight_s, err_3, nothing, 0, 3)
+    for away in range(3, lines):
+        gather_line(0, a_all, away)
+    gather_line(1, left_all, 1)
+    a2a_start(2, both, both_cols, middle_rows, 1, count // 2)
+    a2a_start(3, both, right_a, late_rows, 1, count // 2)
+    take_parts(2, part_2, got_2, support_rows, weight_s, err_3, nothing, 3, 6)
+    gather_line(1, left_all, 2)
+    gather_side(0, a_all)
+    a2a_start(2, both, both_cols, middle_rows, count // 2, count)
+    a2a_start(3, both, right_a, late_rows, count // 2, count)
+    take_parts(2, part_2, got_2, support_rows, weight_s, err_3, nothing, 6, chunks)
 
     back[...] = (acc[...] + dot_of(pairs[...], mixq[...], ((0,), (0,)))).astype(BF)
     rows_mine = rows_all.at[me]
     for h in range(heads):
         late = dot_of(probs_t[:, head(h)], back[:, head(h)], ((1,), (0,)))
         rows_mine[:, head(h)] = ((value_now[:, head(h)] + late) * scale_row).astype(BF)
-    gather_relay_line(1, left_all)
     gather_start(2, rows_all)
-    gather_relay_side(1, left_all)
+    for away in range(3, lines):
+        gather_line(1, left_all, away)
+    gather_side(1, left_all)
 
     x_cols[me] = xf[:, lanes(me * piece, piece)]
-    both_cols[me] = both[:, lanes(me * piece, piece)]
-    err_cols[me] = err_3[:high, lanes(me * piece, piece)]
-
-    a2a_wait(0, xf, x_cols)
-    a2a_wait(1, both, both_cols)
-    gather_finish(0, z_all)
-    gather_relay_line(2, rows_all)
+    both_cols[me] = both[:high, lanes(me * piece, piece)]
+    right_a[me, late_rows] = both[high:, lanes(me * piece, piece)]
+
+    def swap_copy(slot):
+        return remote(swap.at[slot], swap_got.at[slot], swap_sem.at[0, slot], swap_sem.at[1, slot], pair)
+
+    def swap_one(slot):
+        swap[slot] = dot_of(left_all[slot], ow[:, lanes(me * piece, piece)], ((1,), (0,))).astype(BF)
+        swap_copy(slot).start()
+
+    def swap_core(source, carry):
+        swap_one(place(source // 2, lax.rem(source, 2), core))
+        return carry
+
+    def swap_other(source, carry):
+        swap_one(place(source // 2, lax.rem(source, 2), 1 - core))
+        return carry
+
+    lax.fori_loop(0, count // 2, swap_core, 0)
+    gather_line(2, rows_all, 1)
     gather_finish(1, left_all)
+    lax.fori_loop(0, count // 2, swap_other, 0)
+    gather_line(2, rows_all, 2)
+    a2a_wait(0, xf, x_cols, all_rows)
+    a2a_wait(1, err_1, both_cols, early_rows)
+    a2a_wait(2, both, both_cols, middle_rows)
 
     tile = 256
 
     def early(i, carry):
         at = lanes(i * tile, tile)
         do_ref[at, :] = dot_of(
-            left_all[:, :, at].reshape(count * length, tile), both_cols[...].reshape(count * length, piece), ((0,), (0,))
+            left_all[:, :, at].reshape(count * high, tile), both_cols[...].reshape(count * high, piece), ((0,), (0,))
         )
         return carry
     lax.fori_loop(0, width // tile, early, 0)
-    gather_relay_side(2, rows_all)
-    a2a_wait(2, err_3.at[:high], err_cols)
+    for away in range(3, lines):
+        gather_line(2, rows_all, away)
+    a2a_wait(3, both, right_a, late_rows)
+    gather_finish(0, a_all)
+    gather_side(2, rows_all)
+
+    def swapped(slot, carry):
+        swap_copy(slot).wait()
+        right_a[slot, :high] = (swap[slot].astype(F32) + swap_got[slot].astype(F32)).astype(BF)
+        return carry
+    lax.fori_loop(0, count, swapped, 0)
 
     def late_part(i, carry):
         at = lanes(i * tile, tile)
         do_ref[at, :] += dot_of(
-            z_all[:, :, at].reshape(count * high, tile), err_cols[...].reshape(count * high, piece), ((0,), (0,))
+            a_all[:, :, at].reshape(count * length, tile), right_a[...].reshape(count * length, piece), ((0,), (0,))
         )
         return carry
     lax.fori_loop(0, width // tile, late_part, 0)
@@ -559,12 +626,13 @@
         return carry
     lax.fori_loop(0, width // tile, last, 0)
 
+    cross_copy.wait_send()
     for k in range(near):
         x_copy(k, mine).wait_send()
     for number, (send, got) in enumerate(((part_0, got_0), (part_1, got_1), (part_2, got_2))):
         for k in range(chunks):
             part_copy(number, send, got, k, mine).wait_send()
-    for number, array in enumerate((z_all, left_all, rows_all)):
+    for number, array in enumerate((a_all, left_all, rows_all)):
         gather_sent(number, array)
 
 
@@ -576,7 +644,6 @@
     width = queries.shape[1]
     high = 3 * length // 4
     piece = depth // count
-    sends = (lines + 1) + 2 * (lines - 1) + lines
     vm = pltpu.VMEM
     dma = pltpu.SemaphoreType.DMA
     anywhere = pl.BlockSpec(memory_space=pl.ANY)
@@ -596,41 +663,33 @@
             vm((length, width), BF),
             vm((depth, width), BF),
             vm((width, depth), BF),
-            vm((length, width), BF),
-            vm((length, width), BF),
-            vm((length, width), BF),
-            vm((length, width), BF),
-            vm((length, width), BF),
+        ]
+        + [vm((length, width), BF)] * 6
+        + [vm((length, width), F32), vm((length, length), F32)]
+        + [vm((high, depth), BF)] * 6
+        + [vm((length, depth), BF)] * 4
+        + [vm((length, width), BF)]
+        + [vm((length, length), BF)] * 4
+        + [
             vm((length, width), F32),
-            vm((length, length), F32),
-            vm((high, depth), BF),
-            vm((high, depth), BF),
-            vm((high, depth), BF),
-            vm((high, depth), BF),
-            vm((high, depth), BF),
-            vm((high, depth), BF),
-            vm((length, depth), BF),
-            vm((length, depth), BF),
-            vm((length, depth), BF),
-            vm((length, depth), BF),
-            vm((length, width), BF),
-            vm((length, length), BF),
-            vm((length, length), BF),
-            vm((length, length), BF),
-            vm((length, width), F32),
+            vm((high, width), BF),
+            vm((count, length, width), BF),
             vm((count, high, width), BF),
             vm((count, length, width), BF),
-            vm((count, length, width), BF),
             vm((count, length, piece), BF),
+            vm((count, high, piece), BF),
             vm((count, length, piece), BF),
+            vm((count, high, piece), BF),
             vm((count, high, piece), BF),
             dma((6,)),
             dma((2, chunks // 2)),
             dma((3, chunks)),
             dma((3, chunks)),
-            dma((3, count)),
-            dma((3, count)),
-            dma((3, sends)),
+            dma((2,)),
+            dma((2, count)),
+            dma((4, count)),
+            dma((4, count)),
+            dma((3, 5, lines)),
             dma((3, lines)),
             dma((3, lines)),
             dma((3, lines, 2)),

time: 189 us -> 139 us (0.74)
  the two profiles are of different devices: /device:TPU:18 before, /device:TPU:0 now
where the time goes in v2:
time: 139 us
  Pallas kernels  133 us (96%)
  local copies, waits for them, and re-layouts  4.57 us (3%)
    pallas_call x1, Pallas kernels, one_kernel(): pl.pallas_call(functools.partial(step_kernel, lines), out_shape=(jax.Shap...  133 us
    unnamed x2, local copies, waits for them, and re-layouts  4.57 us

profile of v2, /device:TPU:0, one launch (start us, length us, event | category | flops | bytes accessed | tf_op | source)
XLA Modules:
  0.0 139.3 jit_solution(1027610753794924098)
XLA Ops:
  1.3 133.4 %shard_map.86 = (f32[256,1024]{1,0:T(8,128)}, f32[1024,256]{1,0:T(8,128)}) custom-call(bf16[128,2048]{1,0:T(8,128)(2,1)} %x_in.1, bf16[128,2048]{1,0:T(8,128)(2,1)} %t_in.1, bf16[128,1024]{1,0:T(8,128)(2,1)} %q_in.1, bf16[128,1024]{1,0:T(8,128)(2,1)} %k_in.1, bf16[4096,1024]{1,0:T(8,128)(2,1)} %v_in.1, bf16[1024,4096]{1,0:T(8,128)(2,1)} %o_in.1, ...), custom_call_target="tpu_custom_call" | custom-call | tf_op jit(solution)/shard_map/pallas_call | solution.py:651
  134.7 2.3 %copy.12 = f32[256,1024]{1,0:T(8,128)} copy(f32[256,1024]{1,0:T(8,128)} %get-tuple-element.4) | data formatting | bytes 2097152
  137.0 2.3 %copy.13 = f32[1024,256]{1,0:T(8,128)} copy(f32[1024,256]{1,0:T(8,128)} %get-tuple-element.5) | data formatting | bytes 2097152

commit v3 on v2

--- a/solution.py
+++ b/solution.py
@@ -256,7 +256,7 @@
 
     def x_copy(k, owner):
         part = xf.at[:, lanes(owner * half + k * cut, cut)]
-        return remote(part, part, x_sem.at[0, k], x_sem.at[1, k], pair)
+        return remote(part, part, x_sem.at[near], x_sem.at[k], pair)
 
     loads[0].wait()
     for k in range(near):
@@ -267,8 +267,8 @@
         return remote(
             src.at[rows, lanes(peer * piece, piece)],
             dst.at[me, rows],
-            a2a_send.at[number, step],
-            a2a_got.at[number, step],
+            a2a_send.at[number],
+            a2a_got.at[number],
             {"task": peer},
         )
 
@@ -278,29 +278,28 @@
             return carry
         lax.fori_loop(first, last, one, 0)
 
-    def a2a_wait(number, src, dst, rows):
-        def one(step, carry):
-            a2a_copy(number, src, dst, rows, step).wait()
-            return carry
-        lax.fori_loop(1, count, one, 0)
+    def a2a_wait(number, dst, rows):
+        arrived = dst.at[pl.ds(0, count - 1), rows]
+        remote(arrived, arrived, a2a_send.at[number], a2a_got.at[number], {"task": lax.rem(me + 1, count)}).wait()
 
     all_rows = pl.ds(0, length)
 
-    def x_spread(own):
-        def one(step, carry):
-            peer = lax.rem(me + step, count)
-            here = (peer // (count // 2)) == mine
-            @pl.when(here if own else jnp.logical_not(here))
+    def x_spread(owner, first, last):
+        def one(index, carry):
+            step = lax.rem(owner * (count // 2) + index + count - me, count)
+            @pl.when(step > 0)
             def _():
                 a2a_copy(0, xf, x_cols, all_rows, step).start()
             return carry
-        lax.fori_loop(1, count, one, 0)
-
-    x_spread(True)
+        lax.fori_loop(first, last, one, 0)
+
+    x_spread(mine, 0, count // 2)
 
     def gather_copy(number, array, slot, kind, source, got, peer):
-        block = array.at[slot]
-        return remote(block, block, g_send.at[number, kind, source], got, {"task": peer})
+        block = array.at[slot] if number < 3 else array.at[slot, pl.ds(high, length - high)]
+        if number == 0:
+            block = array.at[slot, pl.ds(0, high)]
+        return remote(block, block, g_send.at[number, 0 if kind < 2 else 1], got, {"task": peer})
 
     up_peer, down_peer = me + 4, me - 4
     side_peer, core_peer = place(line, 1 - side, core), place(line, side, 1 - core)
@@ -319,11 +318,10 @@
     def gather_start(number, array):
         pass_on(number, array, line)
 
-    def gather_line(number, array, away):
-        def take(source):
-            slot = place(source, side, core)
-            gather_copy(number, array, slot, 2, source, g_line.at[number, source], side_peer).wait_recv()
-            pass_on(number, array, source)
+    def at_distance(away, take):
+        if away == 0:
+            take(line)
+            return
         @pl.when(line >= away)
         def _():
             take(line - away)
@@ -331,30 +329,47 @@
         def _():
             take(line + away)
 
-    def gather_side(number, array):
-        for source in range(lines):
+    def gather_line(number, array, away):
+        def take(source):
+            slot = place(source, side, core)
+            gather_copy(number, array, slot, 2, source, g_line.at[number, source], side_peer).wait_recv()
+            pass_on(number, array, source)
+        at_distance(away, take)
+
+    def gather_side(number, array, away):
+        def take(source):
             slot = place(source, 1 - side, core)
             gather_copy(number, array, slot, 4, source, g_side.at[number, source], core_peer).wait_recv()
             gather_copy(number, array, slot, 4, source, g_core.at[number, source, 1], core_peer).start()
+        at_distance(away, take)
+
+    def gather_sides(number, array):
+        for away in range(lines):
+            gather_side(number, array, away)
+
+    def gather_core(number, array, source, over):
+        slot = place(source, side if over == 0 else 1 - side, 1 - core)
+        gather_copy(number, array, slot, 3, source, g_core.at[number, source, over], core_peer).wait_recv()
 
     def gather_finish(number, array):
         for source in range(lines):
             for over in range(2):
-                slot = place(source, side if over == 0 else 1 - side, 1 - core)
-                gather_copy(number, array, slot, 3, source, g_core.at[number, source, over], core_peer).wait_recv()
+                gather_core(number, array, source, over)
 
     def gather_sent(number, array):
-        def sent(kind, source):
-            gather_copy(number, array, me, kind, source, g_core.at[number, source, 0], core_peer).wait_send()
-        for source in range(lines):
-            @pl.when(jnp.logical_and(source <= line, line < lines - 1))
+        def sent(blocks, which):
+            rows = (pl.ds(0, high), all_rows, all_rows, pl.ds(high, length - high))[number]
+            if number == 1:
+                rows = pl.ds(0, high)
+            group = array.at[pl.ds(0, blocks), rows]
+            remote(group, group, g_send.at[number, which], g_core.at[number, 0, 0], {"task": core_peer}).wait_send()
+        for at in range(lines):
+            ups = at + 1 if at < lines - 1 else 0
+            downs = lines - at if at > 0 else 0
+            @pl.when(line == at)
             def _():
-                sent(0, source)
-            @pl.when(jnp.logical_and(source >= line, line > 0))
-            def _():
-                sent(1, source)
-            for kind in range(2, 5):
-                sent(kind, source)
+                sent(ups + downs, 0)
+        sent(3 * lines, 1)
 
     def head(h):
         return slice(h * HD, (h + 1) * HD)
@@ -406,10 +421,10 @@
     lax.fori_loop(1, near, own_take, 0)
     def other_take(k, carry):
         x_copy(k, 1 - mine).wait_recv()
+        x_spread(1 - mine, 2 * k, 2 * k + 2)
         take(k, 1 - mine, False)
         return carry
     lax.fori_loop(0, near, other_take, 0)
-    x_spread(False)
 
     gram_raw = half_acc[...]
     diagonal = jnp.where(row == col, gram_raw, F32(0.0))
@@ -423,12 +438,13 @@
         mixed = dot_of(probs[:, head(h)], upper[:, head(h)], ((1,), (0,)))
         z_mine[:, head(h)] = mixed[:high].astype(BF)
     a_mine[:high, :] = (weight_s[:high] * z_mine[...].astype(F32)).astype(BF)
+    gather_start(0, a_all)
     loads[4].wait()
     loads[5].wait()
 
     def part_copy(number, send, got, k, owner):
         at = lanes(lax.rem(owner * near + k, chunks) * cut, cut)
-        return remote(send.at[:, at], got.at[:, at], part_sem.at[number, k], part_got.at[number, k], pair)
+        return remote(send.at[:, at], got.at[:, at], part_sem.at[number], part_got.at[number, k], pair)
 
     def own_columns(k):
         return lanes(lax.rem(mine * near + k, chunks) * cut, cut)
@@ -478,7 +494,9 @@
     early_rows, middle_rows, late_rows = pl.ds(0, low), pl.ds(low, high - low), pl.ds(high, length - high)
     acc[...] = jnp.zeros_like(acc)
     send_parts(0, value_0, support_rows, part_0, got_0, True)
-    take_parts(0, part_0, got_0, support_rows, weight_s, err_1, nothing)
+    take_parts(0, part_0, got_0, support_rows, weight_s, err_1, nothing, 0, 6)
+    gather_line(0, a_all, 1)
+    take_parts(0, part_0, got_0, support_rows, weight_s, err_1, nothing, 6, chunks)
     a2a_start(1, err_1, both_cols, early_rows)
 
     back[...] = acc[...].astype(BF)
@@ -503,14 +521,21 @@
         half_acc[...] += dot_of(part, err_1[:, at], ((1,), (1,)))
 
     send_parts(1, value_1, query_rows, part_1, got_1, True)
+    gather_line(0, a_all, 2)
     cross_copy.wait_recv()
     cross_sum = (cross[...].astype(F32) + cross_got[...].astype(F32)).astype(BF)
     left[...] = (mixq[...].astype(F32) + dot_of(cross_sum[:, :high], a_mine[:high], ((1,), (0,)))).astype(BF)
     a_mine[high:, :] = left[high:, :]
-    gather_start(0, a_all)
-    take_parts(1, part_1, got_1, query_rows, weight_q, err_2, pairs_of, 0, 5)
-    gather_line(0, a_all, 1)
-    take_parts(1, part_1, got_1, query_rows, weight_q, err_2, pairs_of, 5, chunks)
+    gather_start(3, a_all)
+    take_parts(1, part_1, got_1, query_rows, weight_q, err_2, pairs_of, 0, 3)
+    for away in range(3, lines):
+        gather_line(0, a_all, away)
+    take_parts(1, part_1, got_1, query_rows, weight_q, err_2, pairs_of, 3, 5)
+    gather_line(3, a_all, 1)
+    take_parts(1, part_1, got_1, query_rows, weight_q, err_2, pairs_of, 5, 7)
+    gather_sides(0, a_all)
+    take_parts(1, part_1, got_1, query_rows, weight_q, err_2, pairs_of, 7, chunks)
+    gather_line(3, a_all, 2)
 
     pairs[...] = (-step_rate * half_acc[...]).astype(BF)
     back[...] = (acc[...] + dot_of(pairs[:, :high], z_mine[...], ((1,), (0,)))).astype(BF)
@@ -536,18 +561,22 @@
         both[:, at] = jnp.where(is_support, err_1[:, at], err_2[:, at])
         return carry
     lax.fori_loop(0, chunks, join, 0)
-    gather_line(0, a_all, 2)
-    take_parts(2, part_2, got_2, support_rows, weight_s, err_3, nothing, 0, 3)
+    def both_start(first, last):
+        a2a_start(2, both, both_cols, middle_rows, first, last)
+        a2a_start(3, both, right_a, late_rows, first, last)
+
+    both_start(1, 5)
+    take_parts(2, part_2, got_2, support_rows, weight_s, err_3, nothing, 0, 1)
     for away in range(3, lines):
-        gather_line(0, a_all, away)
+        gather_line(3, a_all, away)
+    take_parts(2, part_2, got_2, support_rows, weight_s, err_3, nothing, 1, 2)
     gather_line(1, left_all, 1)
-    a2a_start(2, both, both_cols, middle_rows, 1, count // 2)
-    a2a_start(3, both, right_a, late_rows, 1, count // 2)
-    take_parts(2, part_2, got_2, support_rows, weight_s, err_3, nothing, 3, 6)
+    both_start(5, 10)
+    take_parts(2, part_2, got_2, support_rows, weight_s, err_3, nothing, 2, 4)
+    gather_sides(3, a_all)
+    take_parts(2, part_2, got_2, support_rows, weight_s, err_3, nothing, 4, 6)
     gather_line(1, left_all, 2)
-    gather_side(0, a_all)
-    a2a_start(2, both, both_cols, middle_rows, count // 2, count)
-    a2a_start(3, both, right_a, late_rows, count // 2, count)
+    both_start(10, count)
     take_parts(2, part_2, got_2, support_rows, weight_s, err_3, nothing, 6, chunks)
 
     back[...] = (acc[...] + dot_of(pairs[...], mixq[...], ((0,), (0,)))).astype(BF)
@@ -558,35 +587,39 @@
     gather_start(2, rows_all)
     for away in range(3, lines):
         gather_line(1, left_all, away)
-    gather_side(1, left_all)
+    gather_side(1, left_all, 0)
+    gather_side(1, left_all, 1)
 
     x_cols[me] = xf[:, lanes(me * piece, piece)]
     both_cols[me] = both[:high, lanes(me * piece, piece)]
     right_a[me, late_rows] = both[high:, lanes(me * piece, piece)]
 
     def swap_copy(slot):
-        return remote(swap.at[slot], swap_got.at[slot], swap_sem.at[0, slot], swap_sem.at[1, slot], pair)
+        return remote(swap.at[slot], swap_got.at[slot], swap_sem.at[count], swap_sem.at[slot], pair)
 
     def swap_one(slot):
         swap[slot] = dot_of(left_all[slot], ow[:, lanes(me * piece, piece)], ((1,), (0,))).astype(BF)
         swap_copy(slot).start()
 
-    def swap_core(source, carry):
-        swap_one(place(source // 2, lax.rem(source, 2), core))
-        return carry
-
-    def swap_other(source, carry):
-        swap_one(place(source // 2, lax.rem(source, 2), 1 - core))
-        return carry
-
-    lax.fori_loop(0, count // 2, swap_core, 0)
+    def swap_line(side_at, core_at):
+        def one(source, carry):
+            swap_one(place(source, side_at, core_at))
+            return carry
+        lax.fori_loop(0, lines, one, 0)
+
+    swap_line(side, core)
+    gather_side(1, left_all, 2)
+    for away in range(3, lines):
+        gather_side(1, left_all, away)
     gather_line(2, rows_all, 1)
+    swap_line(1 - side, core)
     gather_finish(1, left_all)
-    lax.fori_loop(0, count // 2, swap_other, 0)
+    swap_line(side, 1 - core)
+    swap_line(1 - side, 1 - core)
     gather_line(2, rows_all, 2)
-    a2a_wait(0, xf, x_cols, all_rows)
-    a2a_wait(1, err_1, both_cols, early_rows)
-    a2a_wait(2, both, both_cols, middle_rows)
+    a2a_wait(0, x_cols, all_rows)
+    a2a_wait(1, both_cols, early_rows)
+    a2a_wait(2, both_cols, middle_rows)
 
     tile = 256
 
@@ -599,12 +632,35 @@
     lax.fori_loop(0, width // tile, early, 0)
     for away in range(3, lines):
         gather_line(2, rows_all, away)
-    a2a_wait(3, both, right_a, late_rows)
+    a2a_wait(3, right_a, late_rows)
     gather_finish(0, a_all)
-    gather_side(2, rows_all)
+    gather_finish(3, a_all)
+
+    def add_pair(source, side_at):
+        both_cores = pl.ds(place(source, side_at, 0), 2)
+        return dot_of(
+            x_cols[both_cores].reshape(2 * length, piece), rows_all[both_cores].reshape(2 * length, width), ((0,), (0,))
+        )
+
+    gather_core(2, rows_all, line, 0)
+    dv_ref[...] = add_pair(line, side)
+
+    def column(source):
+        gather_core(2, rows_all, source, 0)
+        dv_ref[...] += add_pair(source, side)
+
+    def across(source):
+        gather_core(2, rows_all, source, 1)
+        dv_ref[...] += add_pair(source, 1 - side)
+
+    gather_side(2, rows_all, 0)
+    for away in range(1, lines):
+        at_distance(away, column)
+    gather_side(2, rows_all, 1)
+    at_distance(0, across)
 
     def swapped(slot, carry):
-        swap_copy(slot).wait()
+        swap_copy(slot).wait_recv()
         right_a[slot, :high] = (swap[slot].astype(F32) + swap_got[slot].astype(F32)).astype(BF)
         return carry
     lax.fori_loop(0, count, swapped, 0)
@@ -616,23 +672,19 @@
         )
         return carry
     lax.fori_loop(0, width // tile, late_part, 0)
-    gather_finish(2, rows_all)
-
-    def last(i, carry):
-        at = lanes(i * tile, tile)
-        dv_ref[:, at] = dot_of(
-            x_cols[...].reshape(count * length, piece), rows_all[:, :, at].reshape(count * length, tile), ((0,), (0,))
-        )
-        return carry
-    lax.fori_loop(0, width // tile, last, 0)
+    at_distance(1, across)
+    gather_side(2, rows_all, 2)
+    at_distance(2, across)
+    for away in range(3, lines):
+        gather_side(2, rows_all, away)
+        at_distance(away, across)
 
     cross_copy.wait_send()
-    for k in range(near):
-        x_copy(k, mine).wait_send()
+    remote(tg, tg, x_sem.at[near], x_sem.at[0], pair).wait_send()
     for number, (send, got) in enumerate(((part_0, got_0), (part_1, got_1), (part_2, got_2))):
-        for k in range(chunks):
-            part_copy(number, send, got, k, mine).wait_send()
-    for number, array in enumerate((a_all, left_all, rows_all)):
+        remote(send, got, part_sem.at[number], part_got.at[number, 0], pair).wait_send()
+    remote(swap, swap_got, swap_sem.at[count], swap_sem.at[0], pair).wait_send()
+    for number, array in enumerate((a_all, left_all, rows_all, a_all)):
         gather_sent(number, array)
 
 
@@ -651,8 +703,8 @@
     return pl.pallas_call(
         functools.partial(step_kernel, lines),
         out_shape=(
-            jax.ShapeDtypeStruct((piece, width), F32),
-            jax.ShapeDtypeStruct((width, piece), F32),
+            pltpu.VMEM((piece, width), F32),
+            pltpu.VMEM((width, piece), F32),
         ),
         in_specs=[anywhere] * 6 + [pl.BlockSpec(memory_space=pltpu.SMEM)],
         out_specs=(pl.BlockSpec(memory_space=pltpu.VMEM), pl.BlockSpec(memory_space=pltpu.VMEM)),
@@ -682,17 +734,17 @@
             vm((count, high, piece), BF),
             vm((count, high, piece), BF),
             dma((6,)),
-            dma((2, chunks // 2)),
-            dma((3, chunks)),
+            dma((chunks // 2 + 1,)),
+            dma((3,)),
             dma((3, chunks)),
             dma((2,)),
-            dma((2, count)),
-            dma((4, count)),
-            dma((4, count)),
-            dma((3, 5, lines)),
-            dma((3, lines)),
-            dma((3, lines)),
-            dma((3, lines, 2)),
+            dma((count + 1,)),
+            dma((4,)),
+            dma((4,)),
+            dma((4, 2)),
+            dma((4, lines)),
+            dma((4, lines)),
+            dma((4, lines, 2)),
         ],
         compiler_params=pltpu.CompilerParams(
             collective_id=1, has_side_effects=True, vmem_limit_bytes=60 * 2**20

time: 139 us -> 122 us (0.88)
  Pallas kernels: 133 us -> 119 us
  local copies, waits for them, and re-layouts: 4.57 us -> 1.94 us
    pallas_call x1, Pallas kernels: 133 us -> 119 us  [one_kernel(): pl.pallas_call(functools.partial(step_kernel, lines), out_shape=(pltpu.VM...]
    unnamed x2, local copies, waits for them, and re-layouts: 4.57 us -> 1.94 us
where the time goes in v3:
time: 122 us
  Pallas kernels  119 us (98%)
  local copies, waits for them, and re-layouts  1.94 us (2%)
  between operations  1.29 us (1%)
    pallas_call x1, Pallas kernels, one_kernel(): pl.pallas_call(functools.partial(step_kernel, lines), out_shape=(pltpu.VM...  119 us

profile of v3, /device:TPU:0, one launch (start us, length us, event | category | flops | bytes accessed | tf_op | source)
XLA Modules:
  0.0 122.2 jit_solution(10292825865324709247)
XLA Ops:
  1.3 119.0 %shard_map.86 = (f32[256,1024]{1,0:T(8,128)S(1)}, f32[1024,256]{1,0:T(8,128)S(1)}) custom-call(bf16[128,2048]{1,0:T(8,128)(2,1)} %x_in.1, bf16[128,2048]{1,0:T(8,128)(2,1)} %t_in.1, bf16[128,1024]{1,0:T(8,128)(2,1)} %q_in.1, bf16[128,1024]{1,0:T(8,128)(2,1)} %k_in.1, bf16[4096,1024]{1,0:T(8,128)(2,1)} %v_in.1, bf16[1024,4096]{1,0:T(8,128)(2,1)} %o_in.1, ...), custom_call_target="tpu_custom_call" | custom-call | tf_op jit(solution)/shard_map/pallas_call | solution.py:703
  120.3 1.0 copy.11
  121.2 1.0 copy.12

commit v4 on v3

--- a/solution.py
+++ b/solution.py
@@ -295,16 +295,25 @@
 
     x_spread(mine, 0, count // 2)
 
+    part_rows = (pl.ds(0, high), pl.ds(0, high), all_rows, pl.ds(high, length - high), all_rows)
+    part_lanes = (pl.ds(0, width),) * 2 + (pl.ds(0, width // 2), pl.ds(0, width), pl.ds(width // 2, width // 2))
+
     def gather_copy(number, array, slot, kind, source, got, peer):
-        block = array.at[slot] if number < 3 else array.at[slot, pl.ds(high, length - high)]
-        if number == 0:
-            block = array.at[slot, pl.ds(0, high)]
+        block = array.at[slot, part_rows[number], part_lanes[number]]
         return remote(block, block, g_send.at[number, 0 if kind < 2 else 1], got, {"task": peer})
+
+    def from_end(number, source, away):
+        if number in (1, 4) and lines > 2 and away == 2:
+            return jnp.logical_or(source == 0, source == lines - 1)
+        return None
+
+    def detour(number, away):
+        return number == 2 and lines > 2 and away == lines - 1
 
     up_peer, down_peer = me + 4, me - 4
     side_peer, core_peer = place(line, 1 - side, core), place(line, side, 1 - core)
 
-    def pass_on(number, array, source):
+    def pass_on(number, array, source, away):
         slot = place(source, side, core)
         @pl.when(jnp.logical_and(source <= line, line < lines - 1))
         def _():
@@ -312,11 +321,15 @@
         @pl.when(jnp.logical_and(source >= line, line > 0))
         def _():
             gather_copy(number, array, slot, 1, source, g_line.at[number, source], down_peer).start()
-        gather_copy(number, array, slot, 2, source, g_side.at[number, source], side_peer).start()
+        if not detour(number, away):
+            through = from_end(number, source, away)
+            @pl.when(True if through is None else jnp.logical_not(through))
+            def _():
+                gather_copy(number, array, slot, 2, source, g_side.at[number, source], side_peer).start()
         gather_copy(number, array, slot, 3, source, g_core.at[number, source, 0], core_peer).start()
 
     def gather_start(number, array):
-        pass_on(number, array, line)
+        pass_on(number, array, line, 0)
 
     def at_distance(away, take):
         if away == 0:
@@ -333,7 +346,7 @@
         def take(source):
             slot = place(source, side, core)
             gather_copy(number, array, slot, 2, source, g_line.at[number, source], side_peer).wait_recv()
-            pass_on(number, array, source)
+            pass_on(number, array, source, away)
         at_distance(away, take)
 
     def gather_side(number, array, away):
@@ -341,6 +354,15 @@
             slot = place(source, 1 - side, core)
             gather_copy(number, array, slot, 4, source, g_side.at[number, source], core_peer).wait_recv()
             gather_copy(number, array, slot, 4, source, g_core.at[number, source, 1], core_peer).start()
+            through = from_end(number, source, away + 1)
+            if detour(number, away + 1) or through is not None:
+                through = True if through is None else through
+                @pl.when(functools.reduce(jnp.logical_and, (source < line, line < lines - 1, through)))
+                def _():
+                    gather_copy(number, array, slot, 4, source, g_side.at[number, source], up_peer).start()
+                @pl.when(functools.reduce(jnp.logical_and, (source > line, line > 0, through)))
+                def _():
+                    gather_copy(number, array, slot, 4, source, g_side.at[number, source], down_peer).start()
         at_distance(away, take)
 
     def gather_sides(number, array):
@@ -358,18 +380,22 @@
 
     def gather_sent(number, array):
         def sent(blocks, which):
-            rows = (pl.ds(0, high), all_rows, all_rows, pl.ds(high, length - high))[number]
-            if number == 1:
-                rows = pl.ds(0, high)
-            group = array.at[pl.ds(0, blocks), rows]
+            group = array.at[pl.ds(0, blocks), part_rows[number], part_lanes[number]]
             remote(group, group, g_send.at[number, which], g_core.at[number, 0, 0], {"task": core_peer}).wait_send()
         for at in range(lines):
             ups = at + 1 if at < lines - 1 else 0
             downs = lines - at if at > 0 else 0
+            others = 3 * lines
+            if detour(number, lines - 1):
+                ends = (at == 0) + (at == lines - 1)
+                inner = (at == lines - 2) + (at == 1)
+                others += inner - ends
+            if number in (1, 4) and lines > 2:
+                others += (at == 1) + (at == lines - 2) - (at == 2) - (at == lines - 3)
             @pl.when(line == at)
             def _():
                 sent(ups + downs, 0)
-        sent(3 * lines, 1)
+                sent(others, 1)
 
     def head(h):
         return slice(h * HD, (h + 1) * HD)
@@ -561,23 +587,90 @@
         both[:, at] = jnp.where(is_support, err_1[:, at], err_2[:, at])
         return carry
     lax.fori_loop(0, chunks, join, 0)
+    keeper = core == mine
+
     def both_start(first, last):
-        a2a_start(2, both, both_cols, middle_rows, first, last)
-        a2a_start(3, both, right_a, late_rows, first, last)
-
-    both_start(1, 5)
-    take_parts(2, part_2, got_2, support_rows, weight_s, err_3, nothing, 0, 1)
+        def one(index, carry):
+            step = 2 * index + lax.rem(core + mine, 2)
+            @pl.when(step > 0)
+            def _():
+                a2a_copy(2, both, both_cols, middle_rows, step).start()
+                a2a_copy(3, both, right_a, late_rows, step).start()
+            return carry
+        lax.fori_loop(first, last, one, 0)
+
+    def both_moved(number, array, rows, slots):
+        group = array.at[pl.ds(0, slots), rows]
+        return remote(group, group, a2a_send.at[number], a2a_got.at[number], pair)
+
+    both_arrays = ((2, both_cols, middle_rows), (3, right_a, late_rows))
+
+    def both_forward():
+        @pl.when(keeper)
+        def _():
+            both_cols[me, middle_rows] = both[middle_rows, lanes(me * piece, piece)]
+            right_a[me, late_rows] = both[late_rows, lanes(me * piece, piece)]
+            for number, array, rows in both_arrays:
+                both_moved(number, array, rows, count - 1).wait_recv()
+                both_moved(number + 2, array, rows, count).start()
+
+    def both_ready():
+        @pl.when(jnp.logical_not(keeper))
+        def _():
+            for number, array, rows in both_arrays:
+                both_moved(number + 2, array, rows, count).wait_recv()
+
+    def both_sent():
+        @pl.when(keeper)
+        def _():
+            for number, array, rows in both_arrays:
+                both_moved(number, array, rows, count // 2 - 1).wait_send()
+                both_moved(number + 2, array, rows, count).wait_send()
+        @pl.when(jnp.logical_not(keeper))
+        def _():
+            for number, array, rows in both_arrays:
+                both_moved(number, array, rows, count // 2).wait_send()
+
+    def swap_copy(slot):
+        return remote(swap.at[slot], swap_got.at[slot], swap_sem.at[count], swap_sem.at[slot], pair)
+
+    def swap_one(slot):
+        swap[slot] = dot_of(left_all[slot], ow[:, lanes(me * piece, piece)], ((1,), (0,))).astype(BF)
+        swap_copy(slot).start()
+
+    def swap_own(away, over_side):
+        at_distance(away, lambda source: swap_one(place(source, 1 - side if over_side else side, core)))
+
+    def swap_core(away, over):
+        def one(source):
+            gather_core(1, left_all, source, over)
+            swap_one(place(source, 1 - side if over else side, 1 - core))
+        at_distance(away, one)
+
+    def take_2(first, last):
+        take_parts(2, part_2, got_2, support_rows, weight_s, err_3, nothing, first, last)
+
+    both_start(0, 3)
+    take_2(0, 1)
     for away in range(3, lines):
         gather_line(3, a_all, away)
-    take_parts(2, part_2, got_2, support_rows, weight_s, err_3, nothing, 1, 2)
+    swap_own(0, False)
+    take_2(1, 2)
     gather_line(1, left_all, 1)
-    both_start(5, 10)
-    take_parts(2, part_2, got_2, support_rows, weight_s, err_3, nothing, 2, 4)
+    both_start(3, 6)
+    swap_own(1, False)
+    take_2(2, 3)
+    gather_side(1, left_all, 0)
+    swap_own(0, True)
+    take_2(3, 4)
     gather_sides(3, a_all)
-    take_parts(2, part_2, got_2, support_rows, weight_s, err_3, nothing, 4, 6)
+    both_start(6, count // 2)
+    swap_core(0, 0)
+    swap_core(1, 0)
+    take_2(4, 7)
     gather_line(1, left_all, 2)
-    both_start(10, count)
-    take_parts(2, part_2, got_2, support_rows, weight_s, err_3, nothing, 6, chunks)
+    swap_own(2, False)
+    take_2(7, chunks)
 
     back[...] = (acc[...] + dot_of(pairs[...], mixq[...], ((0,), (0,)))).astype(BF)
     rows_mine = rows_all.at[me]
@@ -585,41 +678,67 @@
         late = dot_of(probs_t[:, head(h)], back[:, head(h)], ((1,), (0,)))
         rows_mine[:, head(h)] = ((value_now[:, head(h)] + late) * scale_row).astype(BF)
     gather_start(2, rows_all)
+    gather_start(4, rows_all)
+    gather_side(1, left_all, 1)
+    swap_own(1, True)
+    swap_core(0, 1)
+    swap_core(2, 0)
+    both_forward()
     for away in range(3, lines):
         gather_line(1, left_all, away)
-    gather_side(1, left_all, 0)
-    gather_side(1, left_all, 1)
+        swap_own(away, False)
+    swap_core(1, 1)
 
     x_cols[me] = xf[:, lanes(me * piece, piece)]
-    both_cols[me] = both[:high, lanes(me * piece, piece)]
-    right_a[me, late_rows] = both[high:, lanes(me * piece, piece)]
-
-    def swap_copy(slot):
-        return remote(swap.at[slot], swap_got.at[slot], swap_sem.at[count], swap_sem.at[slot], pair)
-
-    def swap_one(slot):
-        swap[slot] = dot_of(left_all[slot], ow[:, lanes(me * piece, piece)], ((1,), (0,))).astype(BF)
-        swap_copy(slot).start()
-
-    def swap_line(side_at, core_at):
-        def one(source, carry):
-            swap_one(place(source, side_at, core_at))
-            return carry
-        lax.fori_loop(0, lines, one, 0)
-
-    swap_line(side, core)
+    both_cols[me, early_rows] = both[early_rows, lanes(me * piece, piece)]
+
+    def add_pair(number, source, side_at):
+        both_cores = pl.ds(place(source, side_at, 0), 2)
+        return dot_of(
+            x_cols[both_cores].reshape(2 * length, piece),
+            rows_all[both_cores, :, part_lanes[number]].reshape(2 * length, width // 2),
+            ((0,), (0,)),
+        )
+
+    def column(number):
+        def one(source):
+            gather_core(number, rows_all, source, 0)
+            dv_ref[:, part_lanes[number]] += add_pair(number, source, side)
+        return one
+
+    def across(number):
+        def one(source):
+            gather_core(number, rows_all, source, 1)
+            dv_ref[:, part_lanes[number]] += add_pair(number, source, 1 - side)
+        return one
+
+    a2a_wait(0, x_cols, all_rows)
+    gather_line(2, rows_all, 1)
+    for number in (2, 4):
+        gather_core(number, rows_all, line, 0)
+        dv_ref[:, part_lanes[number]] = add_pair(number, line, side)
     gather_side(1, left_all, 2)
+    swap_own(2, True)
+    gather_line(4, rows_all, 1)
+    gather_side(2, rows_all, 0)
+    gather_side(4, rows_all, 0)
+    at_distance(1, column(2))
+    swap_core(2, 1)
+    for away in range(3, lines):
+        swap_core(away, 0)
+    gather_line(2, rows_all, 2)
+    at_distance(1, column(4))
     for away in range(3, lines):
         gather_side(1, left_all, away)
-    gather_line(2, rows_all, 1)
-    swap_line(1 - side, core)
-    gather_finish(1, left_all)
-    swap_line(side, 1 - core)
-    swap_line(1 - side, 1 - core)
-    gather_line(2, rows_all, 2)
-    a2a_wait(0, x_cols, all_rows)
+        swap_own(away, True)
+    gather_line(4, rows_all, 2)
+    at_distance(0, across(2))
+    gather_side(2, rows_all, 1)
+    at_distance(0, across(4))
+    for away in range(3, lines):
+        swap_core(away, 1)
     a2a_wait(1, both_cols, early_rows)
-    a2a_wait(2, both_cols, middle_rows)
+    both_ready()
 
     tile = 256
 
@@ -630,34 +749,22 @@
         )
         return carry
     lax.fori_loop(0, width // tile, early, 0)
+    gather_side(4, rows_all, 1)
+    at_distance(2, column(2))
+    gather_side(2, rows_all, 2)
     for away in range(3, lines):
         gather_line(2, rows_all, away)
-    a2a_wait(3, right_a, late_rows)
+    at_distance(2, column(4))
+    gather_side(4, rows_all, 2)
+    for away in range(3, lines):
+        gather_line(4, rows_all, away)
     gather_finish(0, a_all)
     gather_finish(3, a_all)
-
-    def add_pair(source, side_at):
-        both_cores = pl.ds(place(source, side_at, 0), 2)
-        return dot_of(
-            x_cols[both_cores].reshape(2 * length, piece), rows_all[both_cores].reshape(2 * length, width), ((0,), (0,))
-        )
-
-    gather_core(2, rows_all, line, 0)
-    dv_ref[...] = add_pair(line, side)
-
-    def column(source):
-        gather_core(2, rows_all, source, 0)
-        dv_ref[...] += add_pair(source, side)
-
-    def across(source):
-        gather_core(2, rows_all, source, 1)
-        dv_ref[...] += add_pair(source, 1 - side)
-
-    gather_side(2, rows_all, 0)
-    for away in range(1, lines):
-        at_distance(away, column)
-    gather_side(2, rows_all, 1)
-    at_distance(0, across)
+    for away in range(3, lines):
+        for number in (2, 4):
+            at_distance(away, column(number))
+    for number in (2, 4):
+        at_distance(1, across(number))
 
     def swapped(slot, carry):
         swap_copy(slot).wait_recv()
@@ -672,19 +779,21 @@
         )
         return carry
     lax.fori_loop(0, width // tile, late_part, 0)
-    at_distance(1, across)
-    gather_side(2, rows_all, 2)
-    at_distance(2, across)
+    for number in (2, 4):
+        at_distance(2, across(number))
     for away in range(3, lines):
         gather_side(2, rows_all, away)
-        at_distance(away, across)
+        gather_side(4, rows_all, away)
+        at_distance(away, across(2))
+        at_distance(away, across(4))
 
     cross_copy.wait_send()
+    both_sent()
     remote(tg, tg, x_sem.at[near], x_sem.at[0], pair).wait_send()
     for number, (send, got) in enumerate(((part_0, got_0), (part_1, got_1), (part_2, got_2))):
         remote(send, got, part_sem.at[number], part_got.at[number, 0], pair).wait_send()
     remote(swap, swap_got, swap_sem.at[count], swap_sem.at[0], pair).wait_send()
-    for number, array in enumerate((a_all, left_all, rows_all, a_all)):
+    for number, array in enumerate((a_all, left_all, rows_all, a_all, rows_all)):
         gather_sent(number, array)
 
 
@@ -739,12 +848,12 @@
             dma((3, chunks)),
             dma((2,)),
             dma((count + 1,)),
-            dma((4,)),
-            dma((4,)),
-            dma((4, 2)),
-            dma((4, lines)),
-            dma((4, lines)),
-            dma((4, lines, 2)),
+            dma((6,)),
+            dma((6,)),
+            dma((5, 2)),
+            dma((5, lines)),
+            dma((5, lines)),
+            dma((5, lines, 2)),
         ],
         compiler_params=pltpu.CompilerParams(
             collective_id=1, has_side_effects=True, vmem_limit_bytes=60 * 2**20

time: 122 us -> 115 us (0.943)
  Pallas kernels: 119 us -> 111 us
    pallas_call x1, Pallas kernels: 119 us -> 111 us  [one_kernel(): pl.pallas_call(functools.partial(step_kernel, lines), out_shape=(pltpu.VM...]
where the time goes in v4:
time: 115 us
  Pallas kernels  111 us (97%)
  local copies, waits for them, and re-layouts  1.94 us (2%)
  between operations  1.29 us (1%)
    pallas_call x1, Pallas kernels, one_kernel(): pl.pallas_call(functools.partial(step_kernel, lines), out_shape=(pltpu.VM...  111 us

profile of v4, /device:TPU:0, one launch (start us, length us, event | category | flops | bytes accessed | tf_op | source)
XLA Modules:
  0.0 114.7 jit_solution(13654105088221120813)
XLA Ops:
  1.3 111.5 %shard_map.86 = (f32[256,1024]{1,0:T(8,128)S(1)}, f32[1024,256]{1,0:T(8,128)S(1)}) custom-call(bf16[128,2048]{1,0:T(8,128)(2,1)} %x_in.1, bf16[128,2048]{1,0:T(8,128)(2,1)} %t_in.1, bf16[128,1024]{1,0:T(8,128)(2,1)} %q_in.1, bf16[128,1024]{1,0:T(8,128)(2,1)} %k_in.1, bf16[4096,1024]{1,0:T(8,128)(2,1)} %v_in.1, bf16[1024,4096]{1,0:T(8,128)(2,1)} %o_in.1, ...), custom_call_target="tpu_custom_call" | custom-call | tf_op jit(solution)/shard_map/pallas_call | solution.py:812
  112.7 1.0 copy.11
  113.7 1.0 copy.12

commit v5 on v4

--- a/solution.py
+++ b/solution.py
@@ -200,7 +200,7 @@
     lines,
     x_in, t_in, q_in, k_in, v_in, o_in, split_ref,
     dv_ref, do_ref,
-    xf, tg, qs, ks, vw, ow, probs, probs_t, upper, mixq, second, left, acc, half_acc,
+    xf, tg, qs, ks, vw, ow, probs, probs_t, upper, mixq, second, left, chain, mixed_all, acc, half_acc,
     part_0, part_1, part_2, got_0, got_1, got_2, err_1, err_2, err_3, both,
     back, gram_b, cross, cross_got, pairs, value_now, z_mine, a_all, left_all, rows_all,
     x_cols, both_cols, right_a, swap, swap_got,
@@ -315,17 +315,17 @@
 
     def pass_on(number, array, source, away):
         slot = place(source, side, core)
+        if not detour(number, away):
+            through = from_end(number, source, away)
+            @pl.when(True if through is None else jnp.logical_not(through))
+            def _():
+                gather_copy(number, array, slot, 2, source, g_side.at[number, source], side_peer).start()
         @pl.when(jnp.logical_and(source <= line, line < lines - 1))
         def _():
             gather_copy(number, array, slot, 0, source, g_line.at[number, source], up_peer).start()
         @pl.when(jnp.logical_and(source >= line, line > 0))
         def _():
             gather_copy(number, array, slot, 1, source, g_line.at[number, source], down_peer).start()
-        if not detour(number, away):
-            through = from_end(number, source, away)
-            @pl.when(True if through is None else jnp.logical_not(through))
-            def _():
-                gather_copy(number, array, slot, 2, source, g_side.at[number, source], side_peer).start()
         gather_copy(number, array, slot, 3, source, g_core.at[number, source, 0], core_peer).start()
 
     def gather_start(number, array):
@@ -462,6 +462,7 @@
     a_mine = a_all.at[me]
     for h in range(heads):
         mixed = dot_of(probs[:, head(h)], upper[:, head(h)], ((1,), (0,)))
+        mixed_all[:, head(h)] = mixed
         z_mine[:, head(h)] = mixed[:high].astype(BF)
     a_mine[:high, :] = (weight_s[:high] * z_mine[...].astype(F32)).astype(BF)
     gather_start(0, a_all)
@@ -520,6 +521,9 @@
     early_rows, middle_rows, late_rows = pl.ds(0, low), pl.ds(low, high - low), pl.ds(high, length - high)
     acc[...] = jnp.zeros_like(acc)
     send_parts(0, value_0, support_rows, part_0, got_0, True)
+    for h in range(heads):
+        middle = dot_of(probs[:, head(h)], gram_b[...], ((1,), (0,))).astype(BF)
+        chain[:, head(h)] = (-step_rate * dot_of(middle, probs_t[:, head(h)], ((1,), (0,)))).astype(BF)
     take_parts(0, part_0, got_0, support_rows, weight_s, err_1, nothing, 0, 6)
     gather_line(0, a_all, 1)
     take_parts(0, part_0, got_0, support_rows, weight_s, err_1, nothing, 6, chunks)
@@ -527,9 +531,8 @@
 
     back[...] = acc[...].astype(BF)
     for h in range(heads):
-        up = dot_of(probs_t[:, head(h)], back[:, head(h)], ((1,), (0,))).astype(BF)
-        new = (upper[:, head(h)].astype(F32) - step_rate * dot_of(gram_b[...], up, ((1,), (0,)))).astype(BF)
-        mixq[:, head(h)] = dot_of(probs[:, head(h)], new, ((1,), (0,))).astype(BF)
+        moved = dot_of(chain[:, head(h)], back[:, head(h)], ((1,), (0,)))
+        mixq[:, head(h)] = (mixed_all[:, head(h)] + moved).astype(BF)
     cross[:, high:] = jnp.zeros((length, length - high), BF)
     product = -step_rate * dot_of(mixq[...], z_mine[...], ((1,), (1,)))
     cross[:, :high] = jnp.where(is_support, F32(0.0), product).astype(BF)
@@ -567,10 +570,7 @@
     back[...] = (acc[...] + dot_of(pairs[:, :high], z_mine[...], ((1,), (0,)))).astype(BF)
     left_mine = left_all.at[me]
     for h in range(heads):
-        up = dot_of(probs_t[:, head(h)], back[:, head(h)], ((1,), (0,)))
-        value_now[:, head(h)] = up
-        flow = (-step_rate * dot_of(gram_b[...], up.astype(BF), ((1,), (0,)))).astype(BF)
-        again = dot_of(probs[:, head(h)], flow, ((1,), (0,))).astype(BF)
+        again = dot_of(chain[:, head(h)], back[:, head(h)], ((1,), (0,))).astype(BF)
         second[:, head(h)] = again
         left_mine[:, head(h)] = jnp.where(is_support, again, left[:, head(h)])[:high]
 
@@ -582,6 +582,8 @@
     gather_start(1, left_all)
     send_parts(2, value_2, support_rows, part_2, got_2, False)
 
+    for h in range(heads):
+        value_now[:, head(h)] = dot_of(probs_t[:, head(h)], back[:, head(h)], ((1,), (0,)))
     def join(k, carry):
         at = own_columns(k)
         both[:, at] = jnp.where(is_support, err_1[:, at], err_2[:, at])
@@ -650,26 +652,27 @@
     def take_2(first, last):
         take_parts(2, part_2, got_2, support_rows, weight_s, err_3, nothing, first, last)
 
-    both_start(0, 3)
+    both_start(0, count // 2)
     take_2(0, 1)
     for away in range(3, lines):
         gather_line(3, a_all, away)
     swap_own(0, False)
     take_2(1, 2)
     gather_line(1, left_all, 1)
-    both_start(3, 6)
     swap_own(1, False)
     take_2(2, 3)
     gather_side(1, left_all, 0)
     swap_own(0, True)
     take_2(3, 4)
     gather_sides(3, a_all)
-    both_start(6, count // 2)
     swap_core(0, 0)
     swap_core(1, 0)
-    take_2(4, 7)
+    take_2(4, 5)
     gather_line(1, left_all, 2)
     swap_own(2, False)
+    take_2(5, 7)
+    gather_side(1, left_all, 1)
+    swap_own(1, True)
     take_2(7, chunks)
 
     back[...] = (acc[...] + dot_of(pairs[...], mixq[...], ((0,), (0,)))).astype(BF)
@@ -679,8 +682,6 @@
         rows_mine[:, head(h)] = ((value_now[:, head(h)] + late) * scale_row).astype(BF)
     gather_start(2, rows_all)
     gather_start(4, rows_all)
-    gather_side(1, left_all, 1)
-    swap_own(1, True)
     swap_core(0, 1)
     swap_core(2, 0)
     both_forward()
@@ -755,7 +756,6 @@
     for away in range(3, lines):
         gather_line(2, rows_all, away)
     at_distance(2, column(4))
-    gather_side(4, rows_all, 2)
     for away in range(3, lines):
         gather_line(4, rows_all, away)
     gather_finish(0, a_all)
@@ -763,8 +763,6 @@
     for away in range(3, lines):
         for number in (2, 4):
             at_distance(away, column(number))
-    for number in (2, 4):
-        at_distance(1, across(number))
 
     def swapped(slot, carry):
         swap_copy(slot).wait_recv()
@@ -779,6 +777,9 @@
         )
         return carry
     lax.fori_loop(0, width // tile, late_part, 0)
+    gather_side(4, rows_all, 2)
+    for number in (2, 4):
+        at_distance(1, across(number))
     for number in (2, 4):
         at_distance(2, across(number))
     for away in range(3, lines):
@@ -825,8 +826,9 @@
             vm((depth, width), BF),
             vm((width, depth), BF),
         ]
-        + [vm((length, width), BF)] * 6
-        + [vm((length, width), F32), vm((length, length), F32)]
+        + [vm((length, width), BF)] * 7
+        + [vm((length, width), F32)] * 2
+        + [vm((length, length), F32)]
         + [vm((high, depth), BF)] * 6
         + [vm((length, depth), BF)] * 4
         + [vm((length, width), BF)]

time: 115 us -> 112 us (0.974)
  Pallas kernels: 111 us -> 108 us
    pallas_call x1, Pallas kernels: 111 us -> 108 us  [one_kernel(): pl.pallas_call(functools.partial(step_kernel, lines), out_shape=(pltpu.VM...]
where the time goes in v5:
time: 112 us
  Pallas kernels  108 us (96%)
  local copies, waits for them, and re-layouts  1.94 us (2%)
  between operations  1.29 us (1%)
    pallas_call x1, Pallas kernels, one_kernel(): pl.pallas_call(functools.partial(step_kernel, lines), out_shape=(pltpu.VM...  108 us

profile of v5, /device:TPU:0, one launch (start us, length us, event | category | flops | bytes accessed | tf_op | source)
XLA Modules:
  0.0 111.6 jit_solution(10390503773290279789)
XLA Ops:
  1.3 108.4 %shard_map.86 = (f32[256,1024]{1,0:T(8,128)S(1)}, f32[1024,256]{1,0:T(8,128)S(1)}) custom-call(bf16[128,2048]{1,0:T(8,128)(2,1)} %x_in.1, bf16[128,2048]{1,0:T(8,128)(2,1)} %t_in.1, bf16[128,1024]{1,0:T(8,128)(2,1)} %q_in.1, bf16[128,1024]{1,0:T(8,128)(2,1)} %k_in.1, bf16[4096,1024]{1,0:T(8,128)(2,1)} %v_in.1, bf16[1024,4096]{1,0:T(8,128)(2,1)} %o_in.1, ...), custom_call_target="tpu_custom_call" | custom-call | tf_op jit(solution)/shard_map/pallas_call | solution.py:813
  109.7 1.0 copy.11
  110.7 1.0 copy.12

commit v6 on v5

--- a/solution.py
+++ b/solution.py
@@ -217,6 +217,8 @@
     chunks = 8
     cut = depth // chunks
     near = chunks // 2
+    fine = 2 * near
+    thin = half // fine
 
     me = lax.axis_index("task")
     mine = lax.axis_index("tensor")
@@ -255,11 +257,11 @@
         )
 
     def x_copy(k, owner):
-        part = xf.at[:, lanes(owner * half + k * cut, cut)]
-        return remote(part, part, x_sem.at[near], x_sem.at[k], pair)
+        part = xf.at[:, lanes(owner * half + k * thin, thin)]
+        return remote(part, part, x_sem.at[fine], x_sem.at[k], pair)
 
     loads[0].wait()
-    for k in range(near):
+    for k in range(fine):
         x_copy(k, mine).start()
 
     def a2a_copy(number, src, dst, rows, step):
@@ -429,9 +431,9 @@
     loads[3].wait()
 
     def take(k, owner, first):
-        at = lanes(owner * half + k * cut, cut)
+        at = lanes(owner * half + k * thin, thin)
         x_part = xf[:, at]
-        new = dot_of(x_part, vw[pl.ds(pl.multiple_of(owner * half + k * cut, 128), cut), :], ((1,), (0,)))
+        new = dot_of(x_part, vw[pl.ds(pl.multiple_of(owner * half + k * thin, 128), thin), :], ((1,), (0,)))
         gram = dot_of(x_part, x_part, ((1,), (1,)))
         if first:
             acc[...] = new
@@ -444,13 +446,14 @@
     def own_take(k, carry):
         take(k, mine, False)
         return carry
-    lax.fori_loop(1, near, own_take, 0)
+    lax.fori_loop(1, fine, own_take, 0)
     def other_take(k, carry):
         x_copy(k, 1 - mine).wait_recv()
-        x_spread(1 - mine, 2 * k, 2 * k + 2)
+        each = count // 2 // fine
+        x_spread(1 - mine, each * k, each * (k + 1))
         take(k, 1 - mine, False)
         return carry
-    lax.fori_loop(0, near, other_take, 0)
+    lax.fori_loop(0, fine, other_take, 0)
 
     gram_raw = half_acc[...]
     diagonal = jnp.where(row == col, gram_raw, F32(0.0))
@@ -634,7 +637,7 @@
                 both_moved(number, array, rows, count // 2).wait_send()
 
     def swap_copy(slot):
-        return remote(swap.at[slot], swap_got.at[slot], swap_sem.at[count], swap_sem.at[slot], pair)
+        return remote(swap.at[slot], swap_got.at[slot], swap_sem.at[0], swap_sem.at[1], pair)
 
     def swap_one(slot):
         swap[slot] = dot_of(left_all[slot], ow[:, lanes(me * piece, piece)], ((1,), (0,))).astype(BF)
@@ -764,8 +767,10 @@
         for number in (2, 4):
             at_distance(away, column(number))
 
+    swaps = remote(swap, swap_got, swap_sem.at[0], swap_sem.at[1], pair)
+    swaps.wait_recv()
+
     def swapped(slot, carry):
-        swap_copy(slot).wait_recv()
         right_a[slot, :high] = (swap[slot].astype(F32) + swap_got[slot].astype(F32)).astype(BF)
         return carry
     lax.fori_loop(0, count, swapped, 0)
@@ -790,10 +795,10 @@
 
     cross_copy.wait_send()
     both_sent()
-    remote(tg, tg, x_sem.at[near], x_sem.at[0], pair).wait_send()
+    remote(tg, tg, x_sem.at[fine], x_sem.at[0], pair).wait_send()
     for number, (send, got) in enumerate(((part_0, got_0), (part_1, got_1), (part_2, got_2))):
         remote(send, got, part_sem.at[number], part_got.at[number, 0], pair).wait_send()
-    remote(swap, swap_got, swap_sem.at[count], swap_sem.at[0], pair).wait_send()
+    swaps.wait_send()
     for number, array in enumerate((a_all, left_all, rows_all, a_all, rows_all)):
         gather_sent(number, array)
 
@@ -845,11 +850,11 @@
             vm((count, high, piece), BF),
             vm((count, high, piece), BF),
             dma((6,)),
-            dma((chunks // 2 + 1,)),
+            dma((chunks + 1,)),
             dma((3,)),
             dma((3, chunks)),
             dma((2,)),
-            dma((count + 1,)),
+            dma((2,)),
             dma((6,)),
             dma((6,)),
             dma((5, 2)),
@@ -937,7 +942,7 @@
 
 
 def solution(mesh):
-    whole_step = mesh.shape["tensor"] == 2 and mesh.shape["task"] % 4 == 0
+    whole_step = mesh.shape["tensor"] == 2 and mesh.shape["task"] % 16 == 0
     return jax.shard_map(
         one_kernel if whole_step else make_device(mesh.shape["tensor"]),
         mesh=mesh,

time: 112 us -> 112 us (level)
  no operation moved by 1% of the time
where the time goes in v6:
time: 112 us; the launch traced here: 111 us
  Pallas kernels  108 us (96%)
  local copies, waits for them, and re-layouts  1.94 us (2%)
  between operations  1.29 us (1%)
    pallas_call x1, Pallas kernels, one_kernel(): pl.pallas_call(functools.partial(step_kernel, lines), out_shape=(pltpu.VM...  108 us

profile of v6, /device:TPU:0, one launch (start us, length us, event | category | flops | bytes accessed | tf_op | source)
XLA Modules:
  0.0 111.4 jit_solution(2338417940403743318)
XLA Ops:
  1.3 108.2 %shard_map.86 = (f32[256,1024]{1,0:T(8,128)S(1)}, f32[1024,256]{1,0:T(8,128)S(1)}) custom-call(bf16[128,2048]{1,0:T(8,128)(2,1)} %x_in.1, bf16[128,2048]{1,0:T(8,128)(2,1)} %t_in.1, bf16[128,1024]{1,0:T(8,128)(2,1)} %q_in.1, bf16[128,1024]{1,0:T(8,128)(2,1)} %k_in.1, bf16[4096,1024]{1,0:T(8,128)(2,1)} %v_in.1, bf16[1024,4096]{1,0:T(8,128)(2,1)} %o_in.1, ...), custom_call_target="tpu_custom_call" | custom-call | tf_op jit(solution)/shard_map/pallas_call | solution.py:818
  109.5 1.0 copy.11
  110.5 1.0 copy.12
